TPU v7x, 256 devices: a whole 4x4x8 slice. The times are simulated.
256 devices in a mesh: layer: 16 (over y, x_hi, core), feat: 16 (over z, x_lo).
Axes of the slice: x: 4 (x_hi: 2, x_lo: 2; x = x_hi * 2 + x_lo), y: 4, z: 8, core: 2. Of those that a mesh axis runs over, the one named last changes fastest.
Arguments:
- residual_in: bfloat16 [16, 256, 4096], P('layer', None, 'feat'), may hold values from -6 to 6
- mlp_out: bfloat16 [16, 256, 4096], P('layer', None, 'feat'), may hold values from -6 to 6
- encoder: bfloat16 [16, 4096, 2048], P('layer', None, 'feat'), may hold values from -0.09375 to 0.09375
- encoder_bias: float32 [16, 2048], P('layer', 'feat'), may hold values from -3 to 3
- decoder: bfloat16 [16, 9, 2048, 4096], P('layer', None, 'feat'), may hold values from -0.046875 to 0.046875
- decoder_bias: float32 [16, 4096], P('layer'), may hold values from -3 to 3
Outputs:
- recon_error: bfloat16 [16, 256, 4096], P('layer', None, 'feat')
- pre_grad: float32 [16, 256, 2048], P('layer', None, 'feat')
All inputs are finite; a program needn't handle non-finite values.
Results may differ from a plain program's by a relative error of at most 0.0035.
Values may be sent and summed in bfloat16 or wider, within the bound.
A program may use at most 128 MiB of HBM per device.

v0:
```python
import jax
import jax.numpy as jnp
from jax import lax
from jax.sharding import Mesh
from jax.sharding import PartitionSpec as P

FEAT = ("feat_0", "feat_1")


def sent_to_all(array, axis):
    copies = jnp.broadcast_to(array, (lax.axis_size(axis), *array.shape))
    return lax.all_to_all(copies, axis, split_axis=0, concat_axis=0, tiled=True)


def joined_along(blocks, dim):
    shape = list(blocks.shape[1:])
    shape[dim] *= blocks.shape[0]
    return jnp.moveaxis(blocks, 0, dim).reshape(shape)


def collect(array, axis, dim):
    blocks = sent_to_all(array, axis)
    return joined_along(blocks, dim)


def scatter_axes(array, axes, dim):
    for axis in axes:
        array = lax.psum_scatter(array, axis, scatter_dimension=dim, tiled=True)
    return array


def swapped(array, axis, bit):
    return lax.ppermute(array, axis, [(i, i ^ 1 << bit) for i in range(lax.axis_size(axis))])


def sent_together(arrays, axis, dim, along):
    both = jnp.concatenate(arrays, axis=along)
    whole, at, outs = (lax.all_gather(both, axis, axis=dim, tiled=True), 0, [])
    for a in arrays:
        outs.append(lax.slice_in_dim(whole, at, at + a.shape[along], axis=along))
        at += a.shape[along]
    return tuple(outs)


def in_blocks(array, dim, peers):
    before, after = (array.shape[:dim], array.shape[dim + 1 :])
    return jnp.moveaxis(array.reshape(*before, peers, -1, *after), dim, 0)


def sum_at_owner(array, axis, dim):
    peers = lax.axis_size(axis)
    blocks = lax.all_to_all(in_blocks(array, dim, peers), axis, 0, 0, tiled=True)
    return jnp.sum(blocks, axis=0)


def placement_of(source, layer_row, half_layers, layers):
    own_flag = source <= jnp.minimum(layer_row, half_layers - 1)
    slot_index = jnp.where(own_flag, source, source - half_layers + layer_row + 1)
    over_flag = (
        jnp.logical_not(own_flag) & (source >= half_layers) & (source <= layers - 1 - layer_row)
    )
    return (slot_index, own_flag, over_flag)


def add_source(carry, code_rows, source, layer_row, half_layers, layers, weights):
    slot_index, own_flag, over_flag = placement_of(source, layer_row, half_layers, layers)

    def compute(inner):
        picked = jnp.clip(slot_index, 0, weights.shape[0] - 1)
        block = lax.dynamic_index_in_dim(weights, picked, 0, keepdims=False)
        product = jnp.dot(code_rows, block, preferred_element_type=jnp.float32)
        return (
            inner[0] + jnp.where(own_flag, product, 0.0),
            inner[1] + jnp.where(over_flag, product, 0.0),
        )

    def unchanged(inner):
        return inner

    return lax.cond(own_flag | over_flag, compute, unchanged, carry)


def shards(residual_in, mlp_out, encoder, encoder_bias, decoder, decoder_bias):
    layer_row = lax.axis_index("layer")
    layers = lax.axis_size("layer")
    half_layers = layers // 2
    weights = decoder[0]
    slot_count = weights.shape[0]
    enc_local = encoder[0]
    tokens = residual_in.shape[1]
    model_width = weights.shape[2]
    preact = jnp.dot(
        lax.all_gather(residual_in[0], FEAT, axis=1, tiled=True),
        enc_local,
        preferred_element_type=jnp.float32,
    )
    preact = preact + encoder_bias[0][None, :]
    codes = jnp.maximum(preact, 0.0).astype(jnp.bfloat16)
    empty = jnp.zeros((tokens, model_width), jnp.float32)
    piece = collect(codes[None], "layer", 0)

    def one_row(offset, inner):
        code_rows = lax.dynamic_index_in_dim(piece, offset, 0, keepdims=False)
        return add_source(inner, code_rows, offset, layer_row, half_layers, layers, weights)

    own_part, over_part = lax.fori_loop(0, piece.shape[0], one_row, (empty, empty))
    own_sum, over_sum = (scatter_axes(own_part, FEAT, 1), scatter_axes(over_part, FEAT, 1))
    hops = layers.bit_length() - 1
    for bit in range(hops):
        over_sum = swapped(over_sum, "layer", bit)
    column = lax.axis_index(FEAT)
    share_width = model_width // lax.axis_size(FEAT)
    bias_share = lax.dynamic_slice_in_dim(decoder_bias[0], column * share_width, share_width, 0)
    target_share = mlp_out[0].astype(jnp.float32)
    error_share = (own_sum + over_sum + bias_share[None, :] - target_share).astype(jnp.bfloat16)
    partner_share = error_share
    for bit in range(hops):
        partner_share = swapped(partner_share, "layer", bit)
    error_full, partner_full = sent_together((error_share, partner_share), FEAT, 1, 0)
    slot_ids = jnp.arange(slot_count, dtype=jnp.int32)
    own_slot = slot_ids <= jnp.minimum(layer_row, half_layers - 1)
    slot_errors = jnp.where(own_slot[:, None, None], error_full[None], partner_full[None])
    slot_terms = jnp.einsum(
        "jtd,jfd->jtf", slot_errors, weights, preferred_element_type=jnp.float32
    )
    sources = jnp.arange(layers, dtype=jnp.int32)
    slot_index, own_flag, over_flag = placement_of(sources, layer_row, half_layers, layers)
    picked = jnp.take(slot_terms, jnp.clip(slot_index, 0, slot_count - 1), axis=0)
    by_source = jnp.where((own_flag | over_flag)[:, None, None], picked, 0.0)
    back = sum_at_owner(by_source, "layer", 0)
    return (error_share[None], back)


def solution(mesh):
    split = Mesh(mesh.devices.reshape(mesh.shape["layer"], 8, 2), ("layer", "feat_0", "feat_1"))
    placed = (
        P("layer", None, FEAT),
        P("layer", None, FEAT),
        P("layer", None, FEAT),
        P("layer", FEAT),
        P("layer", None, FEAT, None),
        P("layer", None),
    )
    return jax.shard_map(
        shards,
        mesh=split,
        in_specs=placed,
        out_specs=(P("layer", None, FEAT), P("layer", None, FEAT)),
        check_vma=False,
    )
```

profile of v0, /device:TPU:31, one launch (start us, length us, event | category | flops | bytes accessed | tf_op | source)
XLA Modules:
  0.0 548.7 jit_solution(7001553876224597050)
XLA Ops:
  7.9 72.8 %all-gather.6.cloned.1.call-done = bf16[1,256,4096]{2,1,0:T(8,128)(2,1)} async-done(((bf16[1,256,256]{2,1,0:T(8,128)(2,1)}), bf16[1,256,4096]{2,1,0:T(8,128)(2,1)}) %all-gather.6.cloned.1.call-update) | async-done | bytes 2097168 | tf_op jit(solution)/shard_map/all_gather | solution.py:93
  84.3 21.0 %all-to-all-start = ((bf16[16,1,256,128]{3,2,1,0:T(8,128)(2,1)}), bf16[16,1,256,128]{3,2,1,0:T(8,128)(2,1)S(1)}, u32[]{:S(2)}, u32[]{:S(2)}) async-start(bf16[16,1,256,128]{3,2,1,0:T(8,128)(2,1)} %broadcast_in_dim.69), calls=%async_computation | async-start | bytes 2097152 | tf_op jit(solution)/shard_map/all_to_all | solution.py:12
  105.3 12.9 %all-to-all-done = bf16[16,1,256,128]{3,2,1,0:T(8,128)(2,1)S(1)} async-done(((bf16[16,1,256,128]{3,2,1,0:T(8,128)(2,1)}), bf16[16,1,256,128]{3,2,1,0:T(8,128)(2,1)S(1)}, u32[]{:S(2)}, u32[]{:S(2)}) %all-to-all-start) | async-done | bytes 1048608 | tf_op jit(solution)/shard_map/all_to_all | solution.py:12
  123.1 62.9 %while.17 = (s32[]{:T(128)}, f32[256,4096]{1,0:T(8,128)}, f32[256,4096]{1,0:T(8,128)}, s32[]{:T(128)}, s32[]{:T(128)}, /*index=5*/bf16[16,256,128]{2,1,0:T(8,128...) while((s32[]{:T(128)}, f32[256,4096]{1,0:T(8,128)}, f32[256,4096]{1,0:T(8,128)}, ...), condition=%wide.region_3.4_spmd, body=%wide.region_0.3_spmd.sunk | while | flops 272629760 | bytes 17892716 | solution.py:106
  123.1 7.9 %conditional.2 = ((f32[256,4096]{1,0:T(8,128)}, f32[256,4096]{1,0:T(8,128)})) conditional(s32[]{:T(128)} %convert_element_type.30, (f32[256,4096]{1,0:T(8,128)}, f32[256,4096]{1,0:T(8,128)}) %tuple.62, (pred[]{:T(512)}, s32[]{:T(128)}, bf16[16,256,128]{2,1,0:T(8,128)(2,1)S(1)}, s32[]{:T(128)}, bf16[9,128,4096]{2,1,0:T(8,128)(2,1)}, ...), branch_computations={%region_1.1_spmd, %region_2.2_spmd} | conditional | flops 272629760 | bytes 17892492 | solution.py:80
  123.2 7.9 %select_add_fusion = (f32[256,4096]{1,0:T(8,128)}, f32[256,4096]{1,0:T(8,128)}) fusion(f32[256,4096]{1,0:T(8,128)} %get-tuple-element.269, pred[]{:T(512)} %get-tuple-element.270, f32[256,4096]{1,0:T(8,128)} %get-tuple-element.263, pred[]{:T(512)} %get-tuple-element.264, bf16[9,128,4096]{2,1,0:T(8,128)(2,1)} %get-tuple-element.267, s32[]{:T(128)S(6)} %min.21, ...), kind=kOutput, calls=%fused_computation.1 | convolution fusion | flops 272629760 | bytes 17892360 | tf_op jit(solution)/shard_map/while/body/eval_jaxpr/cond/branch_1_fun/dot_general | solution.py:71
  131.0 7.9 %conditional.2 = ((f32[256,4096]{1,0:T(8,128)}, f32[256,4096]{1,0:T(8,128)})) conditional(s32[]{:T(128)} %convert_element_type.30, (f32[256,4096]{1,0:T(8,128)}, f32[256,4096]{1,0:T(8,128)}) %tuple.62, (pred[]{:T(512)}, s32[]{:T(128)}, bf16[16,256,128]{2,1,0:T(8,128)(2,1)S(1)}, s32[]{:T(128)}, bf16[9,128,4096]{2,1,0:T(8,128)(2,1)}, ...), branch_computations={%region_1.1_spmd, %region_2.2_spmd} | conditional | flops 272629760 | bytes 17892492 | solution.py:80
  131.0 7.8 %select_add_fusion = (f32[256,4096]{1,0:T(8,128)}, f32[256,4096]{1,0:T(8,128)}) fusion(f32[256,4096]{1,0:T(8,128)} %get-tuple-element.269, pred[]{:T(512)} %get-tuple-element.270, f32[256,4096]{1,0:T(8,128)} %get-tuple-element.263, pred[]{:T(512)} %get-tuple-element.264, bf16[9,128,4096]{2,1,0:T(8,128)(2,1)} %get-tuple-element.267, s32[]{:T(128)S(6)} %min.21, ...), kind=kOutput, calls=%fused_computation.1 | convolution fusion | flops 272629760 | bytes 17892360 | tf_op jit(solution)/shard_map/while/body/eval_jaxpr/cond/branch_1_fun/dot_general | solution.py:71
  138.9 7.9 %conditional.2 = ((f32[256,4096]{1,0:T(8,128)}, f32[256,4096]{1,0:T(8,128)})) conditional(s32[]{:T(128)} %convert_element_type.30, (f32[256,4096]{1,0:T(8,128)}, f32[256,4096]{1,0:T(8,128)}) %tuple.62, (pred[]{:T(512)}, s32[]{:T(128)}, bf16[16,256,128]{2,1,0:T(8,128)(2,1)S(1)}, s32[]{:T(128)}, bf16[9,128,4096]{2,1,0:T(8,128)(2,1)}, ...), branch_computations={%region_1.1_spmd, %region_2.2_spmd} | conditional | flops 272629760 | bytes 17892492 | solution.py:80
  138.9 7.9 %select_add_fusion = (f32[256,4096]{1,0:T(8,128)}, f32[256,4096]{1,0:T(8,128)}) fusion(f32[256,4096]{1,0:T(8,128)} %get-tuple-element.269, pred[]{:T(512)} %get-tuple-element.270, f32[256,4096]{1,0:T(8,128)} %get-tuple-element.263, pred[]{:T(512)} %get-tuple-element.264, bf16[9,128,4096]{2,1,0:T(8,128)(2,1)} %get-tuple-element.267, s32[]{:T(128)S(6)} %min.21, ...), kind=kOutput, calls=%fused_computation.1 | convolution fusion | flops 272629760 | bytes 17892360 | tf_op jit(solution)/shard_map/while/body/eval_jaxpr/cond/branch_1_fun/dot_general | solution.py:71
  146.7 7.9 %conditional.2 = ((f32[256,4096]{1,0:T(8,128)}, f32[256,4096]{1,0:T(8,128)})) conditional(s32[]{:T(128)} %convert_element_type.30, (f32[256,4096]{1,0:T(8,128)}, f32[256,4096]{1,0:T(8,128)}) %tuple.62, (pred[]{:T(512)}, s32[]{:T(128)}, bf16[16,256,128]{2,1,0:T(8,128)(2,1)S(1)}, s32[]{:T(128)}, bf16[9,128,4096]{2,1,0:T(8,128)(2,1)}, ...), branch_computations={%region_1.1_spmd, %region_2.2_spmd} | conditional | flops 272629760 | bytes 17892492 | solution.py:80
  146.7 7.8 %select_add_fusion = (f32[256,4096]{1,0:T(8,128)}, f32[256,4096]{1,0:T(8,128)}) fusion(f32[256,4096]{1,0:T(8,128)} %get-tuple-element.269, pred[]{:T(512)} %get-tuple-element.270, f32[256,4096]{1,0:T(8,128)} %get-tuple-element.263, pred[]{:T(512)} %get-tuple-element.264, bf16[9,128,4096]{2,1,0:T(8,128)(2,1)} %get-tuple-element.267, s32[]{:T(128)S(6)} %min.21, ...), kind=kOutput, calls=%fused_computation.1 | convolution fusion | flops 272629760 | bytes 17892360 | tf_op jit(solution)/shard_map/while/body/eval_jaxpr/cond/branch_1_fun/dot_general | solution.py:71
  154.6 7.9 %conditional.2 = ((f32[256,4096]{1,0:T(8,128)}, f32[256,4096]{1,0:T(8,128)})) conditional(s32[]{:T(128)} %convert_element_type.30, (f32[256,4096]{1,0:T(8,128)}, f32[256,4096]{1,0:T(8,128)}) %tuple.62, (pred[]{:T(512)}, s32[]{:T(128)}, bf16[16,256,128]{2,1,0:T(8,128)(2,1)S(1)}, s32[]{:T(128)}, bf16[9,128,4096]{2,1,0:T(8,128)(2,1)}, ...), branch_computations={%region_1.1_spmd, %region_2.2_spmd} | conditional | flops 272629760 | bytes 17892492 | solution.py:80
  154.6 7.9 %select_add_fusion = (f32[256,4096]{1,0:T(8,128)}, f32[256,4096]{1,0:T(8,128)}) fusion(f32[256,4096]{1,0:T(8,128)} %get-tuple-element.269, pred[]{:T(512)} %get-tuple-element.270, f32[256,4096]{1,0:T(8,128)} %get-tuple-element.263, pred[]{:T(512)} %get-tuple-element.264, bf16[9,128,4096]{2,1,0:T(8,128)(2,1)} %get-tuple-element.267, s32[]{:T(128)S(6)} %min.21, ...), kind=kOutput, calls=%fused_computation.1 | convolution fusion | flops 272629760 | bytes 17892360 | tf_op jit(solution)/shard_map/while/body/eval_jaxpr/cond/branch_1_fun/dot_general | solution.py:71
  162.4 7.9 %conditional.2 = ((f32[256,4096]{1,0:T(8,128)}, f32[256,4096]{1,0:T(8,128)})) conditional(s32[]{:T(128)} %convert_element_type.30, (f32[256,4096]{1,0:T(8,128)}, f32[256,4096]{1,0:T(8,128)}) %tuple.62, (pred[]{:T(512)}, s32[]{:T(128)}, bf16[16,256,128]{2,1,0:T(8,128)(2,1)S(1)}, s32[]{:T(128)}, bf16[9,128,4096]{2,1,0:T(8,128)(2,1)}, ...), branch_computations={%region_1.1_spmd, %region_2.2_spmd} | conditional | flops 272629760 | bytes 17892492 | solution.py:80
  162.4 7.8 %select_add_fusion = (f32[256,4096]{1,0:T(8,128)}, f32[256,4096]{1,0:T(8,128)}) fusion(f32[256,4096]{1,0:T(8,128)} %get-tuple-element.269, pred[]{:T(512)} %get-tuple-element.270, f32[256,4096]{1,0:T(8,128)} %get-tuple-element.263, pred[]{:T(512)} %get-tuple-element.264, bf16[9,128,4096]{2,1,0:T(8,128)(2,1)} %get-tuple-element.267, s32[]{:T(128)S(6)} %min.21, ...), kind=kOutput, calls=%fused_computation.1 | convolution fusion | flops 272629760 | bytes 17892360 | tf_op jit(solution)/shard_map/while/body/eval_jaxpr/cond/branch_1_fun/dot_general | solution.py:71
  170.3 7.9 %conditional.2 = ((f32[256,4096]{1,0:T(8,128)}, f32[256,4096]{1,0:T(8,128)})) conditional(s32[]{:T(128)} %convert_element_type.30, (f32[256,4096]{1,0:T(8,128)}, f32[256,4096]{1,0:T(8,128)}) %tuple.62, (pred[]{:T(512)}, s32[]{:T(128)}, bf16[16,256,128]{2,1,0:T(8,128)(2,1)S(1)}, s32[]{:T(128)}, bf16[9,128,4096]{2,1,0:T(8,128)(2,1)}, ...), branch_computations={%region_1.1_spmd, %region_2.2_spmd} | conditional | flops 272629760 | bytes 17892492 | solution.py:80
  170.3 7.9 %select_add_fusion = (f32[256,4096]{1,0:T(8,128)}, f32[256,4096]{1,0:T(8,128)}) fusion(f32[256,4096]{1,0:T(8,128)} %get-tuple-element.269, pred[]{:T(512)} %get-tuple-element.270, f32[256,4096]{1,0:T(8,128)} %get-tuple-element.263, pred[]{:T(512)} %get-tuple-element.264, bf16[9,128,4096]{2,1,0:T(8,128)(2,1)} %get-tuple-element.267, s32[]{:T(128)S(6)} %min.21, ...), kind=kOutput, calls=%fused_computation.1 | convolution fusion | flops 272629760 | bytes 17892360 | tf_op jit(solution)/shard_map/while/body/eval_jaxpr/cond/branch_1_fun/dot_general | solution.py:71
  178.1 7.9 %conditional.2 = ((f32[256,4096]{1,0:T(8,128)}, f32[256,4096]{1,0:T(8,128)})) conditional(s32[]{:T(128)} %convert_element_type.30, (f32[256,4096]{1,0:T(8,128)}, f32[256,4096]{1,0:T(8,128)}) %tuple.62, (pred[]{:T(512)}, s32[]{:T(128)}, bf16[16,256,128]{2,1,0:T(8,128)(2,1)S(1)}, s32[]{:T(128)}, bf16[9,128,4096]{2,1,0:T(8,128)(2,1)}, ...), branch_computations={%region_1.1_spmd, %region_2.2_spmd} | conditional | flops 272629760 | bytes 17892492 | solution.py:80
  178.1 7.8 %select_add_fusion = (f32[256,4096]{1,0:T(8,128)}, f32[256,4096]{1,0:T(8,128)}) fusion(f32[256,4096]{1,0:T(8,128)} %get-tuple-element.269, pred[]{:T(512)} %get-tuple-element.270, f32[256,4096]{1,0:T(8,128)} %get-tuple-element.263, pred[]{:T(512)} %get-tuple-element.264, bf16[9,128,4096]{2,1,0:T(8,128)(2,1)} %get-tuple-element.267, s32[]{:T(128)S(6)} %min.21, ...), kind=kOutput, calls=%fused_computation.1 | convolution fusion | flops 272629760 | bytes 17892360 | tf_op jit(solution)/shard_map/while/body/eval_jaxpr/cond/branch_1_fun/dot_general | solution.py:71
  186.2 62.4 %reduce-scatter.9.cloned.1.call-done = f32[256,512]{1,0:T(8,128)} async-done(((f32[256,4096]{1,0:T(8,128)}), f32[256,512]{1,0:T(8,128)}) %reduce-scatter.9.cloned.1.call-update) | async-done | bytes 524304 | tf_op jit(solution)/shard_map/reduce_scatter | solution.py:28
  249.2 19.5 %reduce-scatter.11.cloned.1.call-done = f32[256,256]{1,0:T(8,128)} async-done(((f32[256,512]{1,0:T(8,128)}), f32[256,256]{1,0:T(8,128)}) %reduce-scatter.11.cloned.1.call-update) | async-done | bytes 262160 | tf_op jit(solution)/shard_map/reduce_scatter | solution.py:28
  269.5 58.6 %reduce-scatter.5.cloned.1.call-done = f32[256,512]{1,0:T(8,128)} async-done(((f32[256,4096]{1,0:T(8,128)}), f32[256,512]{1,0:T(8,128)}) %reduce-scatter.5.cloned.1.call-update) | async-done | bytes 524304 | tf_op jit(solution)/shard_map/reduce_scatter | solution.py:28
  329.5 7.5 %collective-permute-done.1 = f32[256,256]{1,0:T(8,128)S(1)} collective-permute-done((f32[256,256]{1,0:T(8,128)S(1)}, f32[256,256]{1,0:T(8,128)S(1)}, u32[]{:S(2)}, u32[]{:S(2)}) %collective-permute-start.1) | collective-permute-done | bytes 262176 | tf_op jit(solution)/shard_map/ppermute | solution.py:33
  337.5 5.8 %collective-permute-done.2 = f32[256,256]{1,0:T(8,128)S(1)} collective-permute-done((f32[256,256]{1,0:T(8,128)S(1)}, f32[256,256]{1,0:T(8,128)S(1)}, u32[]{:S(2)}, u32[]{:S(2)}) %collective-permute-start.2) | collective-permute-done | bytes 262176 | tf_op jit(solution)/shard_map/ppermute | solution.py:33
  351.4 3.3 collective-permute-start.4
  356.8 5.1 collective-permute-done.5
  362.4 3.3 collective-permute-done.6
  366.8 4.2 collective-permute-done.7
  371.8 113.1 %all-gather.4.cloned.1.call-done = bf16[512,4096]{1,0:T(8,128)(2,1)} async-done(((bf16[512,256]{1,0:T(8,128)(2,1)}), bf16[512,4096]{1,0:T(8,128)(2,1)}) %all-gather.4.cloned.1.call-update) | async-done | bytes 4194320 | tf_op jit(solution)/shard_map/all_gather | solution.py:38
  487.6 8.8 %fusion.6 = f32[9,256,128]{2,1,0:T(8,128)} fusion(pred[9]{0:T(512)(128)(4,1)S(1)} %iota_compare_fusion, bf16[256,4096]{1,0:T(8,128)(2,1)S(1)} %get-tuple-element.307, bf16[256,4096]{1,0:T(8,128)(2,1)S(1)} %get-tuple-element.306, bf16[1,9,128,4096]{3,2,1,0:T(8,128)(2,1)} %bitcast.44), kind=kOutput, calls=%fused_computation.9 | convolution fusion | flops 2425356288 | bytes 14811145 | tf_op jit(solution)/shard_map/jtd,jfd->jtf/dot_general | solution.py:123
  498.8 42.3 %all_to_all.10 = f32[16,1,256,128]{3,2,1,0:T(8,128)S(1)} all-to-all(f32[16,1,256,128]{3,2,1,0:T(8,128)S(1)} %fusion.12), channel_id=1, replica_groups=mesh['layer'=16,'feat_0'=8,'feat_1'=2] {'layer'}, dimensions={0} | all-to-all | bytes 4194304 | tf_op jit(solution)/shard_map/all_to_all | solution.py:52
  (52 shorter events, 31.0 us)
Async XLA Ops:
  7.2 73.6 %copy-start = (bf16[1,4096,128]{2,1,0:T(8,128)(2,1)S(1)}, bf16[1,4096,128]{2,1,0:T(8,128)(2,1)}, u32[]{:S(2)}) copy-start(bf16[1,4096,128]{2,1,0:T(8,128)(2,1)} %param.12) | copy-start | bytes 3145732
  7.2 73.6 %all-gather.6.cloned.1.call-start = ((), (), s32[]{:S(2)}) async-start(), calls=%async_computation.11 | async-start | bytes 2228224 | tf_op jit(solution)/shard_map/all_gather | solution.py:93
  84.3 34.0 %all-to-all-start = ((bf16[16,1,256,128]{3,2,1,0:T(8,128)(2,1)}), bf16[16,1,256,128]{3,2,1,0:T(8,128)(2,1)S(1)}, u32[]{:S(2)}, u32[]{:S(2)}) async-start(bf16[16,1,256,128]{3,2,1,0:T(8,128)(2,1)} %broadcast_in_dim.69), calls=%async_computation | async-start | bytes 2097152 | tf_op jit(solution)/shard_map/all_to_all | solution.py:12
  105.3 143.3 %reduce-scatter.9.cloned.1.call-start = ((), (), s32[]{:S(2)}) async-start(), calls=%async_computation.8 | async-start | bytes 4718592 | tf_op jit(solution)/shard_map/reduce_scatter | solution.py:28
  186.1 164.3 %copy-start.2 = (bf16[1,256,256]{2,1,0:T(8,128)(2,1)S(1)}, bf16[1,256,256]{2,1,0:T(8,128)(2,1)}, u32[]{:S(2)}) copy-start(bf16[1,256,256]{2,1,0:T(8,128)(2,1)} %param.11) | copy-start | bytes 393220
  186.1 82.6 %reduce-scatter.11.cloned.1.call-start = ((), (), s32[]{:S(2)}) async-start(), calls=%async_computation.9 | async-start | bytes 786432 | tf_op jit(solution)/shard_map/reduce_scatter | solution.py:28
  248.6 79.6 %reduce-scatter.5.cloned.1.call-start = ((), (), s32[]{:S(2)}) async-start(), calls=%async_computation.6 | async-start | bytes 4718592 | tf_op jit(solution)/shard_map/reduce_scatter | solution.py:28
  249.1 99.0 %reduce-scatter.7.cloned.1.call-start = ((), (), s32[]{:S(2)}) async-start(), calls=%async_computation.7 | async-start | bytes 786432 | tf_op jit(solution)/shard_map/reduce_scatter | solution.py:28
  268.7 59.6 %collective-permute-start = (f32[256,256]{1,0:T(8,128)}, f32[256,256]{1,0:T(8,128)S(1)}, u32[]{:S(2)}, u32[]{:S(2)}) collective-permute-start(f32[256,256]{1,0:T(8,128)} %reduce-scatter.11.cloned.1.call-done), channel_id=1, source_target_pairs={{0,16},{16,0},{32,48},{48,32},{64,80},{80,64},{96,112},{112,96},{1... | collective-permute-start | bytes 786440 | tf_op jit(solution)/shard_map/ppermute | solution.py:33
  328.2 156.7 %all-gather.4.cloned.1.call-start = ((), (), s32[]{:S(2)}) async-start(), calls=%async_computation.10 | async-start | bytes 4456448 | tf_op jit(solution)/shard_map/all_gather | solution.py:38
  328.2 8.7 %collective-permute-start.1 = (f32[256,256]{1,0:T(8,128)S(1)}, f32[256,256]{1,0:T(8,128)S(1)}, u32[]{:S(2)}, u32[]{:S(2)}) collective-permute-start(f32[256,256]{1,0:T(8,128)S(1)} %collective-permute-done), channel_id=1, source_target_pairs={{0,32},{16,48},{32,0},{48,16},{64,96},{80,112},{96,64},{112,80},{1... | collective-permute-start | bytes 786440 | tf_op jit(solution)/shard_map/ppermute | solution.py:33
  337.0 6.4 %collective-permute-start.2 = (f32[256,256]{1,0:T(8,128)S(1)}, f32[256,256]{1,0:T(8,128)S(1)}, u32[]{:S(2)}, u32[]{:S(2)}) collective-permute-start(f32[256,256]{1,0:T(8,128)S(1)} %collective-permute-done.1), channel_id=1, source_target_pairs={{0,64},{16,80},{32,96},{48,112},{64,0},{80,16},{96,32},{112,48},{1... | collective-permute-start | bytes 786440 | tf_op jit(solution)/shard_map/ppermute | solution.py:33
  343.3 7.0 %collective-permute-start.3 = (f32[256,256]{1,0:T(8,128)S(1)}, f32[256,256]{1,0:T(8,128)S(1)}, u32[]{:S(2)}, u32[]{:S(2)}) collective-permute-start(f32[256,256]{1,0:T(8,128)S(1)} %collective-permute-done.2), channel_id=1, source_target_pairs={{0,128},{16,144},{32,160},{48,176},{64,192},{80,208},{96,224},{112... | collective-permute-start | bytes 786440 | tf_op jit(solution)/shard_map/ppermute | solution.py:33
  351.4 136.2 %copy-start.1 = (bf16[256,256]{1,0:T(8,128)(2,1)}, bf16[256,256]{1,0:T(8,128)(2,1)S(1)}, u32[]{:S(2)}) copy-start(bf16[256,256]{1,0:T(8,128)(2,1)S(1)} %fusion.25) | copy-start | bytes 393220
  351.4 4.3 collective-permute-start.4
  355.7 6.2 %collective-permute-start.5 = (bf16[256,256]{1,0:T(8,128)(2,1)S(1)}, bf16[256,256]{1,0:T(8,128)(2,1)S(1)}, u32[]{:S(2)}, u32[]{:S(2)}) collective-permute-start(bf16[256,256]{1,0:T(8,128)(2,1)S(1)} %collective-permute-done.4), channel_id=1, source_target_pairs={{0,32},{16,48},{32,0},{48,16},{64,96},{80,112},{96,64},{112,80},{1... | collective-permute-start | bytes 393224 | tf_op jit(solution)/shard_map/ppermute | solution.py:33
  361.9 3.8 collective-permute-start.6
  365.7 5.3 collective-permute-start.7
Sparse Core Ops, SparseCore 0:
  9.7 71.0 all-gather.5
  186.2 62.2 reduce-scatter.8
  251.0 17.5 reduce-scatter.10
  271.1 57.0 reduce-scatter.4
  330.5 17.5 reduce-scatter.6
  371.9 112.9 all-gather.3
where the time goes:
time: 553 us; the launch traced here: 549 us
  waiting for transfers between devices  373 us (67%)
  matrix products  73.9 us (13%)
  blocking collectives  42.3 us (8%)
  starting transfers between devices  31.2 us (6%)
  between operations  14.2 us (3%)
  local copies, waits for them, and re-layouts  11.5 us (2%)
    reduce_scatter x4, waiting for transfers between devices, scatter_axes(): array = lax.psum_scatter(array, axis, scatter_dimension=dim, tiled=True)  143 us
    all_gather x1, waiting for transfers between devices, sent_together(): whole, at, outs = (lax.all_gather(both, axis, axis=dim, tiled=True), 0, [])  113 us
    all_gather x1, waiting for transfers between devices, shards(): lax.all_gather(residual_in[0], FEAT, axis=1, tiled=True)  72.8 us
    dot_general x8, matrix products, compute(): product = jnp.dot(code_rows, block, preferred_element_type=jnp.float32)  62.8 us
    all_to_all x1, blocking collectives, sum_at_owner(): lax.all_to_all(in_blocks(array, dim, peers), axis, 0, 0, tiled=True)  42.3 us
    ppermute x8, waiting for transfers between devices, swapped(): lax.ppermute(array, axis, [(i, i ^ 1 << bit) for i in range(lax.axis_size...  29 us
    all_to_all x1, starting transfers between devices, sent_to_all(): return lax.all_to_all(copies, axis, split_axis=0, concat_axis=0, tiled=True)  21 us
    all_to_all x1, waiting for transfers between devices, sent_to_all(): return lax.all_to_all(copies, axis, split_axis=0, concat_axis=0, tiled=True)  12.9 us
  transfers between devices with their start and end apart: 15, of which 14 were waited for; matrix products, arithmetic and copies ran while one was open for 0% of the time, Pallas kernels for 0%

commit v1 on v0

v1 whole, which is shorter than its diff:
```python
import functools

import jax
import jax.numpy as jnp
from jax import lax
from jax.experimental import pallas as pl
from jax.experimental.pallas import tpu as pltpu
from jax.sharding import Mesh
from jax.sharding import PartitionSpec as P

MESH = pl.DeviceIdType.MESH
ZS = 8
FEAT = ("z", "xl")


def around(v, step):
    return lax.rem(v + step + ZS, ZS)


def remote(src, dst, send_sem, recv_sem, **where):
    return pltpu.make_async_remote_copy(
        src_ref=src, dst_ref=dst, send_sem=send_sem, recv_sem=recv_sem, device_id=where, device_id_type=MESH
    )


class Gather:
    def __init__(self, buf, send, recv, z, xl):
        self.buf, self.send, self.recv, self.z, self.xl = buf, send, recv, z, xl
        self.own = 2 * z + xl
        self.other = 2 * z + 1 - xl
        self.up, self.down = around(z, 1), around(z, -1)
        self.sent = []

    def copy(self, way, block):
        where = ({"z": self.up}, {"z": self.down}, {"xl": 1 - self.xl})[way]
        at = self.buf.at[block]
        return remote(at, at, self.send.at[way, block], self.recv.at[block], **where)

    def push(self, way, block):
        self.copy(way, block).start()

    def arrive(self, block):
        self.copy(0, block).wait_recv()

    def begin(self):
        for way in (2, 0, 1):
            self.push(way, self.own)

    def relay(self):
        self.arrive(self.other)
        for way in (0, 1):
            self.push(way, self.other)

    def blocks(self, d):
        out = []
        for col in (0, 1):
            for way in (0, 1):
                if d < 4 or way == col:
                    out.append((way, col, 2 * around(self.z, d if way else -d) + col))
        return out

    def step(self, d):
        for way, col, block in self.blocks(d):
            self.arrive(block)
            if d < 3 or (d == 3 and way == col):
                self.push(way, block)

    def drain(self):
        for way in (0, 1, 2):
            self.copy(way, self.own).wait_send()
        for way in (0, 1):
            self.copy(way, self.other).wait_send()
        for d in (1, 2, 3):
            for way, col, block in self.blocks(d):
                if d < 3 or way == col:
                    self.copy(way, block).wait_send()


def greet(z, xl, me, rows):
    barrier = pltpu.get_barrier_semaphore()
    peers = [{"z": around(z, 1)}, {"z": around(z, -1)}, {"xl": 1 - xl}]
    if rows:
        peers += [{"layer": lax.rem(me + k, rows)} for k in range(1, rows)]
    for peer in peers:
        pl.semaphore_signal(barrier, inc=1, device_id=peer, device_id_type=MESH)
    pl.semaphore_wait(barrier, len(peers))


def encode_kernel(res_ref, enc_ref, bias_ref, codes_ref, buf, acc, send, recv, in_sem):
    z, xl = lax.axis_index("z"), lax.axis_index("xl")
    gather = Gather(buf, send, recv, z, xl)
    load = pltpu.make_async_copy(res_ref, buf.at[gather.own], in_sem)
    load.start()
    greet(z, xl, None, 0)
    load.wait()
    gather.begin()
    width = res_ref.shape[1]

    def add(block):
        rows = pl.ds(pl.multiple_of(block * width, width), width)
        acc[...] += jnp.dot(buf[block], enc_ref[rows, :], preferred_element_type=jnp.float32)

    acc[...] = jnp.zeros_like(acc) + bias_ref[...]
    add(gather.own)
    gather.relay()
    add(gather.other)
    for d in (1, 2, 3, 4):
        gather.step(d)
        for _, _, block in gather.blocks(d):
            add(block)
    codes_ref[...] = jnp.maximum(acc[...], 0.0).astype(codes_ref.dtype)
    gather.drain()


def needs(row, source, layers):
    half = layers // 2
    low = source < half
    wanted = (low & (row >= source)) | (jnp.logical_not(low) & (row <= layers - 1 - source))
    return wanted, jnp.where(low, source, source - (half - 1) + row)


def step_kernel(
    layers,
    codes_ref,
    dec_ref,
    bias_ref,
    mlp_ref,
    err_ref,
    grad_ref,
    weights,
    code_slots,
    rows_in,
    part,
    ring_out,
    ring_in,
    cross_out,
    cross_in,
    mirror_out,
    mirror_in,
    errors,
    terms_out,
    terms_in,
    w_sem,
    code_send,
    code_recv,
    ring_send,
    ring_recv,
    cross_send,
    cross_recv,
    mirror_send,
    mirror_recv,
    back_send,
    gather_send,
    gather_recv,
    term_send,
    term_recv,
):
    half = layers // 2
    me, z, xl = lax.axis_index("layer"), lax.axis_index("z"), lax.axis_index("xl")
    slots, tokens, feats = code_slots.shape
    width = part.shape[3]
    heavy = me < half
    own_slots = jnp.where(heavy, me + 1, half)
    all_slots = jnp.where(heavy, slots, half)
    mirror = layers - 1 - me
    up, down = around(z, 1), around(z, -1)
    mine = 2 * z + xl

    load = pltpu.make_async_copy(dec_ref, weights, w_sem)
    load.start()
    greet(z, xl, me, layers)

    def code_copy(k):
        row = lax.rem(me + k, layers)
        wanted, slot = needs(row, me, layers)
        slot = jnp.where(wanted, slot, 0)
        return wanted, remote(codes_ref, code_slots.at[slot], code_send.at[k], code_recv.at[slot], layer=row)

    for k in range(1, layers):
        wanted, copy = code_copy(k)
        pl.when(wanted)(copy.start)

    @pl.when(heavy)
    def _():
        code_slots[me] = codes_ref[...]

    @pl.when(jnp.logical_not(heavy))
    def _():
        code_slots[slots - 1] = jnp.zeros((tokens, feats), code_slots.dtype)

    for j in range(slots):
        copy = remote(codes_ref, code_slots.at[j], code_send.at[0], code_recv.at[j], layer=mirror)
        pl.when((j < all_slots) & (jnp.logical_not(heavy) | (me != j)))(copy.wait_recv)

    for j in range(slots):
        cols = pl.ds(j * feats, feats)
        block = code_slots[j]
        own = j < own_slots
        rows_in[0, :, cols] = jnp.where(own, block, jnp.zeros_like(block))
        rows_in[1, :, cols] = jnp.where(own, jnp.zeros_like(block), block)
    load.wait()

    def decode(a, blocks):
        for block in blocks:
            cols = pl.ds(pl.multiple_of(block * width, width), width)
            part[a, block] = jnp.dot(rows_in[a], weights[:, cols], preferred_element_type=jnp.float32)

    def target(way, d):
        return around(z, -d if way else d)

    def ring_copy(a, way, j, col):
        return remote(
            ring_out.at[a, way, j, col],
            ring_in.at[a, way, j, col],
            ring_send.at[a, way, j, col],
            ring_recv.at[a, way, j, col],
            z=down if way else up,
        )

    def ring_pieces(j):
        return [(way, col) for col in (0, 1) for way in (0, 1) if j > 0 or way == col]

    def ring_decode(a, j):
        decode(a, [2 * target(way, 4 - j) + col for way, col in ring_pieces(j)])

    def ring_step(a, j):
        before = ring_pieces(j - 1) if j else []
        for way, col in ring_pieces(j):
            value = part[a, 2 * target(way, 4 - j) + col]
            if (way, col) in before:
                ring_copy(a, way, j - 1, col).wait_recv()
                value = value + ring_in[a, way, j - 1, col].astype(jnp.float32)
            ring_out[a, way, j, col] = value.astype(jnp.bfloat16)
            ring_copy(a, way, j, col).start()

    def cross_copy(a):
        return remote(cross_out.at[a], cross_in.at[a], cross_send.at[a], cross_recv.at[a], xl=1 - xl)

    def ring_end(a):
        for col in (0, 1):
            for way in (0, 1):
                ring_copy(a, way, 3, col).wait_recv()

        def total(col):
            both = ring_in[a, 0, 3, col].astype(jnp.float32) + ring_in[a, 1, 3, col].astype(jnp.float32)
            return part[a, 2 * z + col] + both

        cross_out[a] = total(1 - xl).astype(jnp.bfloat16)
        cross_copy(a).start()
        part[a, mine] = total(xl)

    def ring_sum(a):
        cross_copy(a).wait_recv()
        return part[a, mine] + cross_in[a].astype(jnp.float32)

    def mirror_copy():
        return remote(mirror_out, mirror_in, mirror_send, mirror_recv, layer=mirror)

    on_heavy = pl.when(heavy)
    on_light = pl.when(jnp.logical_not(heavy))
    for j in range(4):
        on_heavy(lambda j=j: ring_decode(1, j))
        if j == 0:
            on_heavy(lambda: ring_step(1, 0))
        ring_decode(0, j)
        if j > 0:
            on_heavy(lambda j=j: ring_step(1, j))
        ring_step(0, j)
    on_heavy(lambda: decode(1, [2 * z, 2 * z + 1]))
    decode(0, [2 * z, 2 * z + 1])

    on_heavy(lambda: ring_end(1))
    ring_end(0)

    @on_heavy
    def _():
        mirror_out[...] = ring_sum(1).astype(jnp.bfloat16)
        mirror_copy().start()

    share = ring_sum(0) + bias_ref[pl.ds(mine, 1), :] - mlp_ref[...].astype(jnp.float32)
    part[0, mine] = share

    @on_light
    def _():
        mirror_copy().wait_recv()
        part[0, mine] = part[0, mine] + mirror_in[...].astype(jnp.float32)

    error = part[0, mine].astype(jnp.bfloat16)
    err_ref[...] = error
    errors[0, mine] = error

    gathers = [Gather(errors.at[a], gather_send.at[a], gather_recv.at[a], z, xl) for a in (0, 1)]

    def back_copy():
        return remote(errors.at[0, mine], errors.at[1, mine], back_send, back_recv_sem(), layer=mirror)

    def back_recv_sem():
        return gather_recv.at[1, mine]

    on_light(lambda: back_copy().start())
    first, second = gathers
    first.begin()
    first.relay()
    first.step(1)
    first.step(2)

    @on_heavy
    def _():
        back_copy().wait_recv()
        second.begin()

    first.step(3)
    on_heavy(second.relay)
    first.step(4)
    on_heavy(lambda: second.step(1))

    grad_ref[...] = jnp.zeros_like(grad_ref)

    def term_copy(j):
        source = jnp.where(j < own_slots, j, j + (half - 1) - me)
        return source, remote(
            terms_out.at[j], terms_in.at[me], term_send.at[j], term_recv.at[me], layer=source
        )

    def backward(a):
        def one(j, carry):
            rows = pl.ds(pl.multiple_of(j * feats, feats), feats)
            total = jnp.zeros((tokens, feats), jnp.float32)
            for block in range(2 * ZS):
                total = total + lax.dot_general(
                    errors[a, block],
                    weights[rows, block * width : (block + 1) * width],
                    (((1,), (1,)), ((), ())),
                    preferred_element_type=jnp.float32,
                )
            source, copy = term_copy(j)

            @pl.when(source == me)
            def _():
                grad_ref[...] = total

            @pl.when(source != me)
            def _():
                terms_out[j] = total.astype(terms_out.dtype)
                copy.start()

            return carry

        return one

    lax.fori_loop(0, own_slots, backward(0), 0)

    @on_heavy
    def _():
        second.step(2)
        second.step(3)
        second.step(4)
        lax.fori_loop(own_slots, slots, backward(1), 0)

    def collect(row, carry):
        wanted, _ = needs(row, me, layers)

        @pl.when(wanted & (row != me))
        def _():
            remote(terms_out.at[0], terms_in.at[row], term_send.at[0], term_recv.at[row], layer=mirror).wait_recv()
            grad_ref[...] += terms_in[row].astype(jnp.float32)

        return carry

    lax.fori_loop(0, layers, collect, 0)

    for k in range(1, layers):
        wanted, copy = code_copy(k)
        pl.when(wanted)(copy.wait_send)

    def drain_sums(a):
        for j in range(4):
            for way, col in ring_pieces(j):
                ring_copy(a, way, j, col).wait_send()
        cross_copy(a).wait_send()

    drain_sums(0)
    first.drain()
    on_light(lambda: back_copy().wait_send())

    @on_heavy
    def _():
        drain_sums(1)
        mirror_copy().wait_send()
        second.drain()

    def drain_terms(j, carry):
        source, copy = term_copy(j)
        pl.when(source != me)(copy.wait_send)
        return carry

    lax.fori_loop(0, all_slots, drain_terms, 0)


def shards(residual_in, mlp_out, encoder, encoder_bias, decoder, decoder_bias):
    layers = lax.axis_size("layer")
    tokens, width = residual_in.shape[1:]
    feats = encoder.shape[2]
    slots = decoder.shape[1]
    depth = decoder.shape[3]
    blocks = 2 * ZS
    bf16, f32 = jnp.bfloat16, jnp.float32
    dma = pltpu.SemaphoreType.DMA
    vmem = pl.BlockSpec(memory_space=pltpu.VMEM)
    hbm = pl.BlockSpec(memory_space=pl.ANY)

    codes = pl.pallas_call(
        encode_kernel,
        out_shape=jax.ShapeDtypeStruct((tokens, feats), bf16),
        in_specs=[hbm, vmem, vmem],
        out_specs=vmem,
        scratch_shapes=[
            pltpu.VMEM((blocks, tokens, width), bf16),
            pltpu.VMEM((tokens, feats), f32),
            dma((3, blocks)),
            dma((blocks,)),
            dma,
        ],
        compiler_params=pltpu.CompilerParams(
            collective_id=0, has_side_effects=True, vmem_limit_bytes=16 << 20
        ),
        name="encode",
    )(residual_in[0], encoder[0], encoder_bias)

    error, grad = pl.pallas_call(
        functools.partial(step_kernel, layers),
        out_shape=(
            jax.ShapeDtypeStruct((tokens, width), bf16),
            jax.ShapeDtypeStruct((tokens, feats), f32),
        ),
        in_specs=[vmem, hbm, vmem, vmem],
        out_specs=(vmem, vmem),
        scratch_shapes=[
            pltpu.VMEM((slots * feats, depth), bf16),
            pltpu.VMEM((slots, tokens, feats), bf16),
            pltpu.VMEM((2, tokens, slots * feats), bf16),
            pltpu.VMEM((2, blocks, tokens, width), f32),
            pltpu.VMEM((2, 2, 4, 2, tokens, width), bf16),
            pltpu.VMEM((2, 2, 4, 2, tokens, width), bf16),
            pltpu.VMEM((2, tokens, width), bf16),
            pltpu.VMEM((2, tokens, width), bf16),
            pltpu.VMEM((tokens, width), bf16),
            pltpu.VMEM((tokens, width), bf16),
            pltpu.VMEM((2, blocks, tokens, width), bf16),
            pltpu.VMEM((slots, tokens, feats), bf16),
            pltpu.VMEM((layers, tokens, feats), bf16),
            dma,
            dma((layers,)),
            dma((slots,)),
            dma((2, 2, 4, 2)),
            dma((2, 2, 4, 2)),
            dma((2,)),
            dma((2,)),
            dma,
            dma,
            dma,
            dma((2, 3, blocks)),
            dma((2, blocks)),
            dma((slots,)),
            dma((layers,)),
        ],
        compiler_params=pltpu.CompilerParams(
            collective_id=1, has_side_effects=True, vmem_limit_bytes=56 << 20
        ),
        name="decode_backward",
    )(codes, decoder[0].reshape(slots * feats, depth), decoder_bias.reshape(blocks, width), mlp_out[0])
    return error[None], grad[None]


def solution(mesh):
    split = Mesh(mesh.devices.reshape(mesh.shape["layer"], ZS, 2), ("layer", "z", "xl"))
    placed = (
        P("layer", None, FEAT),
        P("layer", None, FEAT),
        P("layer", None, FEAT),
        P("layer", FEAT),
        P("layer", None, FEAT, None),
        P("layer", None),
    )
    return jax.shard_map(
        shards,
        mesh=split,
        in_specs=placed,
        out_specs=(P("layer", None, FEAT), P("layer", None, FEAT)),
        check_vma=False,
    )
```

time: 553 us -> 169 us (0.31)
  waiting for transfers between devices: 373 us -> 0 us
  Pallas kernels: 0 us -> 159 us
  matrix products: 73.9 us -> 0 us
  blocking collectives: 42.3 us -> 0 us
  starting transfers between devices: 31.2 us -> 0 us
  between operations: 14.2 us -> 0.66 us
    all_gather x2 -> x0, waiting for transfers between devices: 186 us -> none  [the longest x1 113 us: sent_together(): whole, at, outs = (lax.all_gather(both, axis, axis=dim, tiled=True), 0, [])]
    pallas_call x0 -> x2, Pallas kernels: none -> 159 us  [the longest x1 130 us: shards(): pl.pallas_call(functools.partial(step_kernel, layers), out_shape=(jax.Sha...]
    reduce_scatter x4 -> x0, waiting for transfers between devices: 143 us -> none  [scatter_axes(): array = lax.psum_scatter(array, axis, scatter_dimension=dim, tiled=True)]
    dot_general x10 -> x0, matrix products: 73.9 us -> none  [the longest x8 62.8 us: compute(): product = jnp.dot(code_rows, block, preferred_element_type=jnp.float32)]
    all_to_all x1 -> x0, blocking collectives: 42.3 us -> none  [sum_at_owner(): lax.all_to_all(in_blocks(array, dim, peers), axis, 0, 0, tiled=True)]
    ppermute x8 -> x0, waiting for transfers between devices: 29 us -> none  [swapped(): lax.ppermute(array, axis, [(i, i ^ 1 << bit) for i in range(lax.axis_size...]
    all_to_all x1 -> x0, starting transfers between devices: 21 us -> none  [sent_to_all(): return lax.all_to_all(copies, axis, split_axis=0, concat_axis=0, tiled=True)]
    all_to_all x1 -> x0, waiting for transfers between devices: 12.9 us -> none  [sent_to_all(): return lax.all_to_all(copies, axis, split_axis=0, concat_axis=0, tiled=True)]
  transfers between devices with their start and end apart: 15 -> 0, of which waited for: 14 -> 0; matrix products, arithmetic and copies ran while one was open for 0% -> 0% of each run, Pallas kernels for 0% -> 0%
where the time goes in v1:
time: 169 us
  Pallas kernels  159 us (94%)
  local copies, waits for them, and re-layouts  7.67 us (5%)
    pallas_call x1, Pallas kernels, shards(): pl.pallas_call(functools.partial(step_kernel, layers), out_shape=(jax.Sha...  130 us
    pallas_call x1, Pallas kernels, shards(): pl.pallas_call(encode_kernel, out_shape=jax.ShapeDtypeStruct((tokens, fea...  28.7 us
    unnamed x11, local copies, waits for them, and re-layouts  7.05 us

profile of v1, /device:TPU:31, one launch (start us, length us, event | category | flops | bytes accessed | tf_op | source)
XLA Modules:
  0.0 168.7 jit_solution(5642855907971005329)
XLA Ops:
  0.6 0.5 broadcast.3
  1.1 1.4 reduce.3
  2.5 0.6 reshape.7.bias_ref
  3.2 0.0 copy-start
  3.2 1.2 copy-done
  4.4 0.0 copy-start.2
  4.4 0.9 copy-done.2
  5.3 0.0 copy-start.3
  5.3 0.7 copy-done.3
  5.9 28.7 %encode.1.codes_ref = bf16[256,128]{1,0:T(8,128)(2,1)S(1)} custom-call(bf16[256,256]{1,0:T(8,128)(2,1)S(1)} %bitcast.7, bf16[4096,128]{1,0:T(8,128)(2,1)S(1)} %bitcast.6, f32[1,128]{1,0:T(1,128)S(1)} %copy-done.3), custom_call_target="tpu_custom_call" | custom-call | tf_op jit(solution)/shard_map/encode/pallas_call | solution.py:412
  34.7 0.0 copy-start.1
  34.7 0.6 copy-done.1
  35.3 130.2 %decode_backward.1 = (bf16[256,256]{1,0:T(8,128)(2,1)}, f32[256,128]{1,0:T(8,128)}) custom-call(bf16[256,128]{1,0:T(8,128)(2,1)} %copy-done.1, bf16[1152,4096]{1,0:T(8,128)(2,1)} %bitcast.8, f32[16,256]{1,0:T(8,128)} %reshape.7.bias_ref, bf16[256,256]{1,0:T(8,128)(2,1)} %bitcast.9), custom_call_target="tpu_custom_call" | custom-call | tf_op jit(solution)/shard_map/decode_backward/pallas_call | solution.py:430
  165.6 1.6 copy.10
  167.2 1.6 copy.11
Async XLA Ops:
  3.2 1.2 copy-start
  4.4 0.9 copy-start.2
  5.3 0.7 copy-start.3
  34.7 0.6 copy-start.1

commit v2 on v0

v2 whole, which is shorter than its diff:
```python
import functools

import jax
import jax.numpy as jnp
from jax import lax
from jax.experimental import pallas as pl
from jax.experimental.pallas import tpu as pltpu
from jax.sharding import Mesh
from jax.sharding import PartitionSpec as P

MESH = pl.DeviceIdType.MESH
ZS = 8
FEAT = ("z", "xl")
LEAD = 1


def around(v, step):
    return lax.rem(v + step + ZS, ZS)


def remote(src, dst, send_sem, recv_sem, **where):
    return pltpu.make_async_remote_copy(
        src_ref=src, dst_ref=dst, send_sem=send_sem, recv_sem=recv_sem, device_id=where, device_id_type=MESH
    )


class Gather:
    def __init__(self, buf, send, recv, z, xl, turn):
        self.buf, self.send, self.recv, self.z, self.xl, self.turn = buf, send, recv, z, xl, turn
        self.own = 2 * z + xl
        self.other = 2 * z + 1 - xl
        self.up, self.down = around(z, 1), around(z, -1)

    def copy(self, way, block):
        where = ({"z": self.up}, {"z": self.down}, {"xl": 1 - self.xl})[way]
        at = self.buf.at[block]
        return remote(at, at, self.send.at[way, block], self.recv.at[block], **where)

    def push(self, way, block):
        self.copy(way, block).start()

    def arrive(self, block):
        self.copy(0, block).wait_recv()

    def begin(self):
        for way in (2, 0, 1):
            self.push(way, self.own)

    def drain_own(self):
        for way in (0, 1, 2):
            self.copy(way, self.own).wait_send()


class Wide(Gather):
    def relay(self):
        self.arrive(self.other)
        for way in (0, 1):
            self.push(way, self.other)
        return [self.other]

    def blocks(self, d):
        out = []
        for col in (0, 1):
            for way in (0, 1):
                if d < 4 or way == col:
                    out.append((way, col, 2 * around(self.z, d if way else -d) + col))
        return out

    def step(self, d):
        for way, col, block in self.blocks(d):
            self.arrive(block)
            if d < 3 or (d == 3 and way == col):
                self.push(way, block)
        return [block for _, _, block in self.blocks(d)]

    def phases(self):
        return [self.relay] + [functools.partial(self.step, d) for d in (1, 2, 3, 4)]

    def drain(self):
        self.drain_own()
        for way in (0, 1):
            self.copy(way, self.other).wait_send()
        for d in (1, 2, 3):
            for way, col, block in self.blocks(d):
                if d < 3 or way == col:
                    self.copy(way, block).wait_send()


class Narrow(Gather):
    def blocks(self, d):
        if d == 4:
            return [(None, 2 * around(self.z, 4) + self.xl)]
        return [(way, 2 * around(self.z, d if way else -d) + self.xl) for way in (0, 1)]

    def crossed(self, d):
        places = [self.z] if d == 0 else [around(self.z, 4)] if d == 4 else [around(self.z, -d), around(self.z, d)]
        return [2 * place + 1 - self.xl for place in places]

    def step(self, d):
        out = []
        if d < 5:
            for way, block in self.blocks(d):
                self.arrive(block)
                if d < 3:
                    self.push(way, block)
                if d == 3:
                    pl.when(self.turn == way)(self.copy(way, block).start)
                self.push(2, block)
                out.append(block)
        for block in self.crossed(d - 1):
            self.arrive(block)
            out.append(block)
        return out

    def phases(self):
        return [functools.partial(self.step, d) for d in (1, 2, 3, 4, 5)]

    def drain(self):
        self.drain_own()
        for d in (1, 2, 3, 4):
            for way, block in self.blocks(d):
                if d < 3:
                    self.copy(way, block).wait_send()
                if d == 3:
                    pl.when(self.turn == way)(self.copy(way, block).wait_send)
                self.copy(2, block).wait_send()


def needs(row, source, layers):
    half = layers // 2
    low = source < half
    wanted = (low & (row >= source)) | (jnp.logical_not(low) & (row <= layers - 1 - source))
    return wanted, jnp.where(low, source, source - (half - 1) + row)


def step_kernel(
    layers,
    res_ref,
    mlp_ref,
    enc_ref,
    enc_bias_ref,
    dec_ref,
    dec_bias_ref,
    err_ref,
    grad_ref,
    residual,
    mlp,
    encoder,
    enc_bias,
    weights,
    dec_bias,
    preact,
    codes,
    code_slots,
    rows_in,
    part,
    ring_out,
    ring_in,
    cross_out,
    cross_in,
    hand_out,
    hand_in,
    mirror_out,
    mirror_in,
    errors,
    terms_out,
    terms_in,
    load_sem,
    res_send,
    res_recv,
    code_send,
    code_recv,
    ring_send,
    ring_recv,
    cross_send,
    cross_recv,
    hand_send,
    hand_recv,
    mirror_send,
    mirror_recv,
    back_send,
    gather_send,
    gather_recv,
    term_send,
    term_recv,
):
    half = layers // 2
    me, z, xl = lax.axis_index("layer"), lax.axis_index("z"), lax.axis_index("xl")
    _, slots, tokens, feats = code_slots.shape
    width = part.shape[4]
    bf16, f32 = jnp.bfloat16, jnp.float32
    heavy = me < half
    own_slots = jnp.where(heavy, me + 1, half)
    all_slots = jnp.where(heavy, slots, half)
    mirror = layers - 1 - me
    turn = lax.rem(me, 2)
    up, down = around(z, 1), around(z, -1)
    mine = 2 * z + xl
    on_heavy = pl.when(heavy)
    on_light = pl.when(jnp.logical_not(heavy))

    loads = [
        pltpu.make_async_copy(res_ref.at[pl.ds(h * tokens, tokens)], residual.at[h, mine], load_sem.at[h]) for h in (0, 1)
    ]
    loads += [
        pltpu.make_async_copy(enc_ref, encoder, load_sem.at[2]),
        pltpu.make_async_copy(enc_bias_ref, enc_bias, load_sem.at[3]),
        pltpu.make_async_copy(dec_ref, weights, load_sem.at[4]),
        pltpu.make_async_copy(mlp_ref, mlp, load_sem.at[5]),
        pltpu.make_async_copy(dec_bias_ref, dec_bias, load_sem.at[6]),
    ]
    for load in loads:
        load.start()

    barrier = pltpu.get_barrier_semaphore()
    peers = [{"z": up}, {"z": down}, {"xl": 1 - xl}]
    peers += [{"layer": lax.rem(me + k, layers)} for k in range(1, layers)]
    for peer in peers:
        pl.semaphore_signal(barrier, inc=1, device_id=peer, device_id_type=MESH)
    pl.semaphore_wait(barrier, len(peers))

    drains = []

    def stream(h):
        wide = h == 0
        kind = Wide if wide else Narrow
        here = pl.ds(h * tokens, tokens)

        inputs = kind(residual.at[h], res_send.at[h], res_recv.at[h], z, xl, turn)
        loads[h].wait()
        inputs.begin()
        yield

        if wide:
            loads[2].wait()
            loads[3].wait()

        def encode(blocks):
            total = preact[h]
            for block in blocks:
                rows = pl.ds(pl.multiple_of(block * width, width), width)
                total = total + jnp.dot(residual[h, block], encoder[rows, :], preferred_element_type=f32)
            preact[h] = total

        preact[h] = jnp.zeros((tokens, feats), f32) + enc_bias[...]
        encode([inputs.own])
        for phase in inputs.phases():
            encode(phase())
            yield
        codes[h] = jnp.maximum(preact[h], 0.0).astype(bf16)

        def code_copy(k):
            row = lax.rem(me + k, layers)
            wanted, slot = needs(row, me, layers)
            slot = jnp.where(wanted, slot, 0)
            copy = remote(codes.at[h], code_slots.at[h, slot], code_send.at[h, k], code_recv.at[h, slot], layer=row)
            return wanted, copy

        for k in range(1, layers):
            wanted, copy = code_copy(k)
            pl.when(wanted)(copy.start)

        @on_heavy
        def _():
            code_slots[h, me] = codes[h]

        @on_light
        def _():
            code_slots[h, slots - 1] = jnp.zeros((tokens, feats), bf16)

        yield
        for j in range(slots):
            copy = remote(codes.at[h], code_slots.at[h, j], code_send.at[h, 0], code_recv.at[h, j], layer=mirror)
            pl.when((j < all_slots) & (jnp.logical_not(heavy) | (me != j)))(copy.wait_recv)
        for j in range(slots):
            cols = pl.ds(j * feats, feats)
            block = code_slots[h, j]
            own = j < own_slots
            rows_in[h, 0, :, cols] = jnp.where(own, block, jnp.zeros_like(block))
            rows_in[h, 1, :, cols] = jnp.where(own, jnp.zeros_like(block), block)
        if wide:
            for load in loads[4:]:
                load.wait()

        def decode(a, block):
            cols = pl.ds(pl.multiple_of(block * width, width), width)
            part[h, a, block] = jnp.dot(rows_in[h, a], weights[:, cols], preferred_element_type=f32)

        def target(way, d):
            return around(z, jnp.where(way == 0, d, -d))

        def ring_copy(a, way, j, col):
            at = (h, a, way, j, col)
            return remote(
                ring_out.at[at], ring_in.at[at], ring_send.at[at], ring_recv.at[at], z=jnp.where(way == 0, up, down)
            )

        def cross_copy(a):
            return remote(cross_out.at[a], cross_in.at[a], cross_send.at[a], cross_recv.at[a], xl=1 - xl)

        def hand_copy(a, place):
            return remote(
                hand_out.at[a, place], hand_in.at[a, place], hand_send.at[a, place], hand_recv.at[a, place], xl=1 - xl
            )

        def ring_pieces(j):
            if wide:
                return [(way, col) for col in (0, 1) for way in (0, 1) if j > 0 or way == col]
            return [(turn, 0)] if j == 0 else [(turn, 0), (1 - turn, 0)]

        def block_of(way, d, col):
            return 2 * target(way, d) + (col if wide else xl)

        def hand_over(a):
            for place in [around(z, s) for s in (4, 3, -3, 2, -2, 1, -1, 0)]:
                block = 2 * place + 1 - xl
                decode(a, block)
                hand_out[a, place] = part[h, a, block].astype(bf16)
                hand_copy(a, place).start()

        def ring_decode(a, j):
            for way, col in ring_pieces(j):
                decode(a, block_of(way, 4 - j, col))

        def ring_step(a, j):
            before = ring_pieces(j - 1) if j else []
            for n, (way, col) in enumerate(ring_pieces(j)):
                place = target(way, 4 - j)
                value = part[h, a, block_of(way, 4 - j, col)]
                if not wide:
                    hand_copy(a, place).wait_recv()
                    value = value + hand_in[a, place].astype(f32)
                if (way, col) in before if wide else n < len(before):
                    ring_copy(a, way, j - 1, col).wait_recv()
                    value = value + ring_in[h, a, way, j - 1, col].astype(f32)
                ring_out[h, a, way, j, col] = value.astype(bf16)
                ring_copy(a, way, j, col).start()

        def ring_end(a):
            for col in (0, 1) if wide else (0,):
                for way in (0, 1):
                    ring_copy(a, way, 3, col).wait_recv()

            def total(block, col):
                both = ring_in[h, a, 0, 3, col].astype(f32) + ring_in[h, a, 1, 3, col].astype(f32)
                return part[h, a, block] + both

            if wide:
                cross_out[a] = total(2 * z + 1 - xl, 1 - xl).astype(bf16)
                cross_copy(a).start()
                part[h, a, mine] = total(mine, xl)
            else:
                hand_copy(a, z).wait_recv()
                part[h, a, mine] = total(mine, 0) + hand_in[a, z].astype(f32)

        def ring_sum(a):
            if wide:
                cross_copy(a).wait_recv()
                return part[h, a, mine] + cross_in[a].astype(f32)
            return part[h, a, mine]

        def mirror_copy():
            return remote(mirror_out.at[h], mirror_in.at[h], mirror_send.at[h], mirror_recv.at[h], layer=mirror)

        if not wide:
            on_heavy(lambda: hand_over(1))
            yield
            hand_over(0)
        for j in range(4):
            on_heavy(lambda: ring_decode(1, j))
            on_heavy(lambda: ring_step(1, j))
            yield
            ring_decode(0, j)
            ring_step(0, j)
            yield
        for a in (1, 0):
            def last(a=a):
                decode(a, mine)
                if wide:
                    decode(a, 2 * z + 1 - xl)
                ring_end(a)

            if a:
                on_heavy(last)
            else:
                last()
            yield

        @on_heavy
        def _():
            mirror_out[h] = ring_sum(1).astype(bf16)
            mirror_copy().start()

        yield
        bias = dec_bias[:, pl.ds(pl.multiple_of(mine * width, width), width)]
        part[h, 0, mine] = ring_sum(0) + bias - mlp[here, :].astype(f32)

        @on_light
        def _():
            mirror_copy().wait_recv()
            part[h, 0, mine] = part[h, 0, mine] + mirror_in[h].astype(f32)

        error = part[h, 0, mine].astype(bf16)
        err_ref[here, :] = error
        errors[h, 0, mine] = error

        first, second = [
            kind(errors.at[h, a], gather_send.at[h, a], gather_recv.at[h, a], z, xl, turn) for a in (0, 1)
        ]

        def back_copy():
            return remote(
                errors.at[h, 0, mine], errors.at[h, 1, mine], back_send.at[h], gather_recv.at[h, 1, mine], layer=mirror
            )

        on_light(lambda: back_copy().start())
        first.begin()
        yield
        early, late = first.phases(), second.phases()
        for phase in early[:3]:
            phase()
            yield

        @on_heavy
        def _():
            back_copy().wait_recv()
            second.begin()

        yield
        early[3]()
        yield
        on_heavy(lambda: late[0]() and None)
        yield
        early[4]()
        yield
        on_heavy(lambda: late[1]() and None)
        yield

        grad_ref[here, :] = jnp.zeros((tokens, feats), f32)

        def term_copy(j):
            source = jnp.where(j < own_slots, j, j + (half - 1) - me)
            return source, remote(
                terms_out.at[h, j], terms_in.at[h, me], term_send.at[h, j], term_recv.at[h, me], layer=source
            )

        def backward(a):
            def one(j, carry):
                rows = pl.ds(pl.multiple_of(j * feats, feats), feats)
                total = jnp.zeros((tokens, feats), f32)
                for block in range(2 * ZS):
                    total = total + lax.dot_general(
                        errors[h, a, block],
                        weights[rows, block * width : (block + 1) * width],
                        (((1,), (1,)), ((), ())),
                        preferred_element_type=f32,
                    )
                source, copy = term_copy(j)

                @pl.when(source == me)
                def _():
                    grad_ref[here, :] = total

                @pl.when(source != me)
                def _():
                    terms_out[h, j] = total.astype(bf16)
                    copy.start()

                return carry

            return one

        lax.fori_loop(0, own_slots, backward(0), 0)
        yield
        for phase in late[2:]:
            on_heavy(lambda phase=phase: phase() and None)
            yield

        @on_heavy
        def _():
            lax.fori_loop(own_slots, slots, backward(1), 0)

        yield

        def collect(row, carry):
            wanted, _ = needs(row, me, layers)

            @pl.when(wanted & (row != me))
            def _():
                remote(
                    terms_out.at[h, 0], terms_in.at[h, row], term_send.at[h, 0], term_recv.at[h, row], layer=mirror
                ).wait_recv()
                grad_ref[here, :] += terms_in[h, row].astype(f32)

            return carry

        lax.fori_loop(0, layers, collect, 0)

        def drain():
            inputs.drain()
            for k in range(1, layers):
                wanted, copy = code_copy(k)
                pl.when(wanted)(copy.wait_send)

            def drain_sums(a):
                for j in range(4):
                    for way, col in ring_pieces(j):
                        ring_copy(a, way, j, col).wait_send()
                if wide:
                    cross_copy(a).wait_send()
                else:
                    for place in range(ZS):
                        hand_copy(a, place).wait_send()

            drain_sums(0)
            first.drain()
            on_light(lambda: back_copy().wait_send())

            @on_heavy
            def _():
                drain_sums(1)
                mirror_copy().wait_send()
                second.drain()

            def drain_terms(j, carry):
                source, copy = term_copy(j)
                pl.when(source != me)(copy.wait_send)
                return carry

            lax.fori_loop(0, all_slots, drain_terms, 0)

        drains.append(drain)

    running = [stream(0), stream(1)]
    for _ in range(LEAD):
        next(running[0])
    while running:
        for s in list(running):
            try:
                next(s)
            except StopIteration:
                running.remove(s)
    for drain in drains:
        drain()


def shards(residual_in, mlp_out, encoder, encoder_bias, decoder, decoder_bias):
    layers = lax.axis_size("layer")
    tokens, width = residual_in.shape[1:]
    feats = encoder.shape[2]
    slots = decoder.shape[1]
    depth = decoder.shape[3]
    blocks = 2 * ZS
    part = tokens // 2
    bf16, f32 = jnp.bfloat16, jnp.float32
    dma, vmem = pltpu.SemaphoreType.DMA, pltpu.VMEM

    error, grad = pl.pallas_call(
        functools.partial(step_kernel, layers),
        out_shape=(
            jax.ShapeDtypeStruct((tokens, width), bf16),
            jax.ShapeDtypeStruct((tokens, feats), f32),
        ),
        in_specs=[pl.BlockSpec(memory_space=pltpu.HBM)] * 6,
        out_specs=(pl.BlockSpec(memory_space=vmem),) * 2,
        scratch_shapes=[
            vmem((2, blocks, part, width), bf16),
            vmem((tokens, width), bf16),
            vmem((depth, feats), bf16),
            vmem((1, feats), f32),
            vmem((slots * feats, depth), bf16),
            vmem((1, depth), f32),
            vmem((2, part, feats), f32),
            vmem((2, part, feats), bf16),
            vmem((2, slots, part, feats), bf16),
            vmem((2, 2, part, slots * feats), bf16),
            vmem((2, 2, blocks, part, width), f32),
            vmem((2, 2, 2, 4, 2, part, width), bf16),
            vmem((2, 2, 2, 4, 2, part, width), bf16),
            vmem((2, part, width), bf16),
            vmem((2, part, width), bf16),
            vmem((2, ZS, part, width), bf16),
            vmem((2, ZS, part, width), bf16),
            vmem((2, part, width), bf16),
            vmem((2, part, width), bf16),
            vmem((2, 2, blocks, part, width), bf16),
            vmem((2, slots, part, feats), bf16),
            vmem((2, layers, part, feats), bf16),
            dma((7,)),
            dma((2, 3, blocks)),
            dma((2, blocks)),
            dma((2, layers)),
            dma((2, slots)),
            dma((2, 2, 2, 4, 2)),
            dma((2, 2, 2, 4, 2)),
            dma((2,)),
            dma((2,)),
            dma((2, ZS)),
            dma((2, ZS)),
            dma((2,)),
            dma((2,)),
            dma((2,)),
            dma((2, 2, 3, blocks)),
            dma((2, 2, blocks)),
            dma((2, slots)),
            dma((2, layers)),
        ],
        compiler_params=pltpu.CompilerParams(
            collective_id=0, has_side_effects=True, vmem_limit_bytes=60 << 20
        ),
        name="transcoder_step",
    )(residual_in[0], mlp_out[0], encoder[0], encoder_bias, decoder[0].reshape(slots * feats, depth), decoder_bias)
    return error[None], grad[None]


def solution(mesh):
    split = Mesh(mesh.devices.reshape(mesh.shape["layer"], ZS, 2), ("layer", "z", "xl"))
    placed = (
        P("layer", None, FEAT),
        P("layer", None, FEAT),
        P("layer", None, FEAT),
        P("layer", FEAT),
        P("layer", None, FEAT, None),
        P("layer", None),
    )
    return jax.shard_map(
        shards,
        mesh=split,
        in_specs=placed,
        out_specs=(P("layer", None, FEAT), P("layer", None, FEAT)),
        check_vma=False,
    )
```

time: 553 us -> 148 us (0.27)
  waiting for transfers between devices: 373 us -> 0 us
  Pallas kernels: 0 us -> 144 us
  matrix products: 73.9 us -> 0 us
  blocking collectives: 42.3 us -> 0 us
  starting transfers between devices: 31.2 us -> 0 us
  between operations: 14.2 us -> 0.64 us
  local copies, waits for them, and re-layouts: 11.5 us -> 3.14 us
    all_gather x2 -> x0, waiting for transfers between devices: 186 us -> none  [the longest x1 113 us: sent_together(): whole, at, outs = (lax.all_gather(both, axis, axis=dim, tiled=True), 0, [])]
    pallas_call x0 -> x1, Pallas kernels: none -> 144 us  [shards(): pl.pallas_call(functools.partial(step_kernel, layers), out_shape=(jax.Sha...]
    reduce_scatter x4 -> x0, waiting for transfers between devices: 143 us -> none  [scatter_axes(): array = lax.psum_scatter(array, axis, scatter_dimension=dim, tiled=True)]
    dot_general x10 -> x0, matrix products: 73.9 us -> none  [the longest x8 62.8 us: compute(): product = jnp.dot(code_rows, block, preferred_element_type=jnp.float32)]
    all_to_all x1 -> x0, blocking collectives: 42.3 us -> none  [sum_at_owner(): lax.all_to_all(in_blocks(array, dim, peers), axis, 0, 0, tiled=True)]
    ppermute x8 -> x0, waiting for transfers between devices: 29 us -> none  [swapped(): lax.ppermute(array, axis, [(i, i ^ 1 << bit) for i in range(lax.axis_size...]
    all_to_all x1 -> x0, starting transfers between devices: 21 us -> none  [sent_to_all(): return lax.all_to_all(copies, axis, split_axis=0, concat_axis=0, tiled=True)]
    all_to_all x1 -> x0, waiting for transfers between devices: 12.9 us -> none  [sent_to_all(): return lax.all_to_all(copies, axis, split_axis=0, concat_axis=0, tiled=True)]
  transfers between devices with their start and end apart: 15 -> 0, of which waited for: 14 -> 0; matrix products, arithmetic and copies ran while one was open for 0% -> 0% of each run, Pallas kernels for 0% -> 0%
where the time goes in v2:
time: 148 us; the launch traced here: 147 us
  Pallas kernels  144 us (97%)
  local copies, waits for them, and re-layouts  3.14 us (2%)
    pallas_call x1, Pallas kernels, shards(): pl.pallas_call(functools.partial(step_kernel, layers), out_shape=(jax.Sha...  144 us
    unnamed x2, local copies, waits for them, and re-layouts  3.14 us

profile of v2, /device:TPU:31, one launch (start us, length us, event | category | flops | bytes accessed | tf_op | source)
XLA Modules:
  0.0 147.3 jit_solution(7200114518636420019)
XLA Ops:
  0.6 143.5 %transcoder_step.1 = (bf16[256,256]{1,0:T(8,128)(2,1)}, f32[256,128]{1,0:T(8,128)}) custom-call(bf16[256,256]{1,0:T(8,128)(2,1)} %bitcast.8, bf16[256,256]{1,0:T(8,128)(2,1)} %bitcast.9, bf16[4096,128]{1,0:T(8,128)(2,1)} %bitcast.7, f32[1,128]{1,0:T(1,128)} %enc_bias_ref.1, bf16[1152,4096]{1,0:T(8,128)(2,1)} %bitcast.6, f32[1,4096]{1,0:T(1,128)} %dec_bias_ref.1), custom_call_target="tpu_custom_call" | custom-call | tf_op jit(solution)/shard_map/transcoder_step/pallas_call | solution.py:558
  144.2 1.6 %copy.10 = bf16[1,256,256]{2,1,0:T(8,128)(2,1)} copy(bf16[1,256,256]{2,1,0:T(8,128)(2,1)} %bitcast.11) | data formatting | bytes 262144
  145.8 1.6 %copy.11 = f32[1,256,128]{2,1,0:T(8,128)} copy(f32[1,256,128]{2,1,0:T(8,128)} %bitcast.10) | data formatting | bytes 262144

commit v3 on v2

--- a/solution.py
+++ b/solution.py
@@ -11,7 +11,7 @@
 MESH = pl.DeviceIdType.MESH
 ZS = 8
 FEAT = ("z", "xl")
-LEAD = 1
+ORDER = 25 * "AB" + "BAB"
 
 
 def around(v, step):
@@ -34,7 +34,7 @@
     def copy(self, way, block):
         where = ({"z": self.up}, {"z": self.down}, {"xl": 1 - self.xl})[way]
         at = self.buf.at[block]
-        return remote(at, at, self.send.at[way, block], self.recv.at[block], **where)
+        return remote(at, at, self.send, self.recv.at[block], **where)
 
     def push(self, way, block):
         self.copy(way, block).start()
@@ -46,9 +46,9 @@
         for way in (2, 0, 1):
             self.push(way, self.own)
 
-    def drain_own(self):
-        for way in (0, 1, 2):
-            self.copy(way, self.own).wait_send()
+    def drain(self):
+        sent = self.buf.at[pl.ds(0, 2 * ZS - 1)]
+        remote(sent, sent, self.send, self.recv.at[0], z=self.up).wait_send()
 
 
 class Wide(Gather):
@@ -73,17 +73,11 @@
                 self.push(way, block)
         return [block for _, _, block in self.blocks(d)]
 
+    def ready(self, n):
+        return [block for _, _, block in self.blocks(n)] if n else [self.other]
+
     def phases(self):
         return [self.relay] + [functools.partial(self.step, d) for d in (1, 2, 3, 4)]
-
-    def drain(self):
-        self.drain_own()
-        for way in (0, 1):
-            self.copy(way, self.other).wait_send()
-        for d in (1, 2, 3):
-            for way, col, block in self.blocks(d):
-                if d < 3 or way == col:
-                    self.copy(way, block).wait_send()
 
 
 class Narrow(Gather):
@@ -112,18 +106,11 @@
             out.append(block)
         return out
 
+    def ready(self, n):
+        return ([block for _, block in self.blocks(n + 1)] if n < 4 else []) + self.crossed(n)
+
     def phases(self):
         return [functools.partial(self.step, d) for d in (1, 2, 3, 4, 5)]
-
-    def drain(self):
-        self.drain_own()
-        for d in (1, 2, 3, 4):
-            for way, block in self.blocks(d):
-                if d < 3:
-                    self.copy(way, block).wait_send()
-                if d == 3:
-                    pl.when(self.turn == way)(self.copy(way, block).wait_send)
-                self.copy(2, block).wait_send()
 
 
 def needs(row, source, layers):
@@ -163,6 +150,7 @@
     mirror_out,
     mirror_in,
     errors,
+    sums,
     terms_out,
     terms_in,
     load_sem,
@@ -191,7 +179,6 @@
     bf16, f32 = jnp.bfloat16, jnp.float32
     heavy = me < half
     own_slots = jnp.where(heavy, me + 1, half)
-    all_slots = jnp.where(heavy, slots, half)
     mirror = layers - 1 - me
     turn = lax.rem(me, 2)
     up, down = around(z, 1), around(z, -1)
@@ -244,16 +231,17 @@
 
         preact[h] = jnp.zeros((tokens, feats), f32) + enc_bias[...]
         encode([inputs.own])
-        for phase in inputs.phases():
+        for n, phase in enumerate(inputs.phases()):
             encode(phase())
-            yield
+            if n < 4:
+                yield
         codes[h] = jnp.maximum(preact[h], 0.0).astype(bf16)
 
         def code_copy(k):
             row = lax.rem(me + k, layers)
             wanted, slot = needs(row, me, layers)
             slot = jnp.where(wanted, slot, 0)
-            copy = remote(codes.at[h], code_slots.at[h, slot], code_send.at[h, k], code_recv.at[h, slot], layer=row)
+            copy = remote(codes.at[h], code_slots.at[h, slot], code_send.at[h, k], code_recv.at[h], layer=row)
             return wanted, copy
 
         for k in range(1, layers):
@@ -269,22 +257,33 @@
             code_slots[h, slots - 1] = jnp.zeros((tokens, feats), bf16)
 
         yield
-        for j in range(slots):
-            copy = remote(codes.at[h], code_slots.at[h, j], code_send.at[h, 0], code_recv.at[h, j], layer=mirror)
-            pl.when((j < all_slots) & (jnp.logical_not(heavy) | (me != j)))(copy.wait_recv)
+        got = code_slots.at[h, pl.ds(0, half)]
+        remote(got, got, code_send.at[h, 0], code_recv.at[h], layer=mirror).wait_recv()
         for j in range(slots):
             cols = pl.ds(j * feats, feats)
             block = code_slots[h, j]
             own = j < own_slots
-            rows_in[h, 0, :, cols] = jnp.where(own, block, jnp.zeros_like(block))
-            rows_in[h, 1, :, cols] = jnp.where(own, jnp.zeros_like(block), block)
+            rows_in[h, 0:tokens, cols] = jnp.where(own, block, jnp.zeros_like(block))
+            rows_in[h, tokens:, cols] = jnp.where(own, jnp.zeros_like(block), block)
         if wide:
             for load in loads[4:]:
                 load.wait()
 
-        def decode(a, block):
-            cols = pl.ds(pl.multiple_of(block * width, width), width)
-            part[h, a, block] = jnp.dot(rows_in[h, a], weights[:, cols], preferred_element_type=f32)
+        def decode(blocks):
+            def columns(block):
+                return weights[:, pl.ds(pl.multiple_of(block * width, width), width)]
+
+            @on_heavy
+            def _():
+                for block in blocks:
+                    both = jnp.dot(rows_in[h], columns(block), preferred_element_type=f32)
+                    part[h, 0, block] = both[:tokens]
+                    part[h, 1, block] = both[tokens:]
+
+            @on_light
+            def _():
+                for block in blocks:
+                    part[h, 0, block] = jnp.dot(rows_in[h, 0:tokens, :], columns(block), preferred_element_type=f32)
 
         def target(way, d):
             return around(z, jnp.where(way == 0, d, -d))
@@ -292,7 +291,7 @@
         def ring_copy(a, way, j, col):
             at = (h, a, way, j, col)
             return remote(
-                ring_out.at[at], ring_in.at[at], ring_send.at[at], ring_recv.at[at], z=jnp.where(way == 0, up, down)
+                ring_out.at[at], ring_in.at[at], ring_send.at[h, a], ring_recv.at[at], z=jnp.where(way == 0, up, down)
             )
 
         def cross_copy(a):
@@ -300,7 +299,7 @@
 
         def hand_copy(a, place):
             return remote(
-                hand_out.at[a, place], hand_in.at[a, place], hand_send.at[a, place], hand_recv.at[a, place], xl=1 - xl
+                hand_out.at[a, place], hand_in.at[a, place], hand_send.at[a], hand_recv.at[a, place], xl=1 - xl
             )
 
         def ring_pieces(j):
@@ -311,16 +310,20 @@
         def block_of(way, d, col):
             return 2 * target(way, d) + (col if wide else xl)
 
-        def hand_over(a):
-            for place in [around(z, s) for s in (4, 3, -3, 2, -2, 1, -1, 0)]:
-                block = 2 * place + 1 - xl
-                decode(a, block)
-                hand_out[a, place] = part[h, a, block].astype(bf16)
-                hand_copy(a, place).start()
-
-        def ring_decode(a, j):
-            for way, col in ring_pieces(j):
-                decode(a, block_of(way, 4 - j, col))
+        def hand_over(steps):
+            places = [around(z, s) for s in steps]
+            decode([2 * place + 1 - xl for place in places])
+
+            def send(a):
+                for place in places:
+                    hand_out[a, place] = part[h, a, 2 * place + 1 - xl].astype(bf16)
+                    hand_copy(a, place).start()
+
+            on_heavy(lambda: send(1))
+            send(0)
+
+        def ring_decode(j):
+            decode([block_of(way, 4 - j, col) for way, col in ring_pieces(j)])
 
         def ring_step(a, j):
             before = ring_pieces(j - 1) if j else []
@@ -363,28 +366,18 @@
             return remote(mirror_out.at[h], mirror_in.at[h], mirror_send.at[h], mirror_recv.at[h], layer=mirror)
 
         if not wide:
-            on_heavy(lambda: hand_over(1))
+            hand_over((4, 3, -3))
             yield
-            hand_over(0)
+            hand_over((2, -2, 1, -1, 0))
         for j in range(4):
-            on_heavy(lambda: ring_decode(1, j))
+            ring_decode(j)
             on_heavy(lambda: ring_step(1, j))
-            yield
-            ring_decode(0, j)
             ring_step(0, j)
             yield
-        for a in (1, 0):
-            def last(a=a):
-                decode(a, mine)
-                if wide:
-                    decode(a, 2 * z + 1 - xl)
-                ring_end(a)
-
-            if a:
-                on_heavy(last)
-            else:
-                last()
-            yield
+        decode([mine, 2 * z + 1 - xl] if wide else [mine])
+        on_heavy(lambda: ring_end(1))
+        ring_end(0)
+        yield
 
         @on_heavy
         def _():
@@ -416,6 +409,43 @@
         on_light(lambda: back_copy().start())
         first.begin()
         yield
+        def term_copy(j):
+            source = jnp.where(j < own_slots, j, j + (half - 1) - me)
+            return source, remote(
+                terms_out.at[h, j], terms_in.at[h, me], term_send.at[h], term_recv.at[h, me], layer=source
+            )
+
+        def backward(a, blocks, start, end):
+            def one(j, carry):
+                rows = pl.ds(pl.multiple_of(j * feats, feats), feats)
+                total = jnp.zeros((tokens, feats), f32) if start else sums[h, j]
+                for block in blocks:
+                    cols = pl.ds(pl.multiple_of(block * width, width), width)
+                    total = total + lax.dot_general(
+                        errors[h, a, block],
+                        weights[rows, cols],
+                        (((1,), (1,)), ((), ())),
+                        preferred_element_type=f32,
+                    )
+                if not end:
+                    sums[h, j] = total
+                    return carry
+                source, copy = term_copy(j)
+
+                @pl.when(source == me)
+                def _():
+                    grad_ref[here, :] = total
+
+                @pl.when(source != me)
+                def _():
+                    terms_out[h, j] = total.astype(bf16)
+                    copy.start()
+
+                return carry
+
+            lax.fori_loop(own_slots if a else 0, slots if a else own_slots, one, 0)
+
+        grad_ref[here, :] = jnp.zeros((tokens, feats), f32)
         early, late = first.phases(), second.phases()
         for phase in early[:3]:
             phase()
@@ -429,56 +459,40 @@
         yield
         early[3]()
         yield
-        on_heavy(lambda: late[0]() and None)
+
+        @on_heavy
+        def _():
+            late[0]()
+
         yield
         early[4]()
         yield
-        on_heavy(lambda: late[1]() and None)
-        yield
-
-        grad_ref[here, :] = jnp.zeros((tokens, feats), f32)
-
-        def term_copy(j):
-            source = jnp.where(j < own_slots, j, j + (half - 1) - me)
-            return source, remote(
-                terms_out.at[h, j], terms_in.at[h, me], term_send.at[h, j], term_recv.at[h, me], layer=source
-            )
-
-        def backward(a):
-            def one(j, carry):
-                rows = pl.ds(pl.multiple_of(j * feats, feats), feats)
-                total = jnp.zeros((tokens, feats), f32)
-                for block in range(2 * ZS):
-                    total = total + lax.dot_general(
-                        errors[h, a, block],
-                        weights[rows, block * width : (block + 1) * width],
-                        (((1,), (1,)), ((), ())),
-                        preferred_element_type=f32,
-                    )
-                source, copy = term_copy(j)
-
-                @pl.when(source == me)
-                def _():
-                    grad_ref[here, :] = total
-
-                @pl.when(source != me)
-                def _():
-                    terms_out[h, j] = total.astype(bf16)
-                    copy.start()
-
-                return carry
-
-            return one
-
-        lax.fori_loop(0, own_slots, backward(0), 0)
-        yield
-        for phase in late[2:]:
-            on_heavy(lambda phase=phase: phase() and None)
-            yield
-
-        @on_heavy
-        def _():
-            lax.fori_loop(own_slots, slots, backward(1), 0)
+
+        @on_heavy
+        def _():
+            late[1]()
+            backward(1, [second.own] + second.ready(0) + second.ready(1), True, False)
+
+        yield
+        backward(0, list(range(2 * ZS)), True, True)
+        yield
+
+        @on_heavy
+        def _():
+            late[2]()
+
+        yield
+
+        @on_heavy
+        def _():
+            late[3]()
+            backward(1, second.ready(2) + second.ready(3), False, False)
+
+        yield
+
+        @on_heavy
+        def _():
+            backward(1, late[4](), False, True)
 
         yield
 
@@ -488,7 +502,7 @@
             @pl.when(wanted & (row != me))
             def _():
                 remote(
-                    terms_out.at[h, 0], terms_in.at[h, row], term_send.at[h, 0], term_recv.at[h, row], layer=mirror
+                    terms_out.at[h, 0], terms_in.at[h, row], term_send.at[h], term_recv.at[h, row], layer=mirror
                 ).wait_recv()
                 grad_ref[here, :] += terms_in[h, row].astype(f32)
 
@@ -503,14 +517,13 @@
                 pl.when(wanted)(copy.wait_send)
 
             def drain_sums(a):
-                for j in range(4):
-                    for way, col in ring_pieces(j):
-                        ring_copy(a, way, j, col).wait_send()
+                sent = residual.at[h, pl.ds(0, 14 if wide else 7)]
+                remote(sent, sent, ring_send.at[h, a], ring_recv.at[h, a, 0, 0, 0], z=up).wait_send()
                 if wide:
                     cross_copy(a).wait_send()
                 else:
-                    for place in range(ZS):
-                        hand_copy(a, place).wait_send()
+                    sent = hand_out.at[a]
+                    remote(sent, sent, hand_send.at[a], hand_recv.at[a, 0], xl=1 - xl).wait_send()
 
             drain_sums(0)
             first.drain()
@@ -522,24 +535,15 @@
                 mirror_copy().wait_send()
                 second.drain()
 
-            def drain_terms(j, carry):
-                source, copy = term_copy(j)
-                pl.when(source != me)(copy.wait_send)
-                return carry
-
-            lax.fori_loop(0, all_slots, drain_terms, 0)
+            sent = terms_out.at[h, pl.ds(0, half)]
+            remote(sent, sent, term_send.at[h], term_recv.at[h, 0], layer=mirror).wait_send()
 
         drains.append(drain)
 
-    running = [stream(0), stream(1)]
-    for _ in range(LEAD):
-        next(running[0])
-    while running:
-        for s in list(running):
-            try:
-                next(s)
-            except StopIteration:
-                running.remove(s)
+    running = {"A": stream(0), "B": stream(1)}
+    for name in ORDER + 40 * "AB":
+        if name in running and next(running[name], "end") == "end":
+            del running[name]
     for drain in drains:
         drain()
 
@@ -573,7 +577,7 @@
             vmem((2, part, feats), f32),
             vmem((2, part, feats), bf16),
             vmem((2, slots, part, feats), bf16),
-            vmem((2, 2, part, slots * feats), bf16),
+            vmem((2, tokens, slots * feats), bf16),
             vmem((2, 2, blocks, part, width), f32),
             vmem((2, 2, 2, 4, 2, part, width), bf16),
             vmem((2, 2, 2, 4, 2, part, width), bf16),
@@ -584,25 +588,26 @@
             vmem((2, part, width), bf16),
             vmem((2, part, width), bf16),
             vmem((2, 2, blocks, part, width), bf16),
+            vmem((2, slots, part, feats), f32),
             vmem((2, slots, part, feats), bf16),
             vmem((2, layers, part, feats), bf16),
             dma((7,)),
-            dma((2, 3, blocks)),
+            dma((2,)),
             dma((2, blocks)),
             dma((2, layers)),
-            dma((2, slots)),
+            dma((2,)),
+            dma((2, 2)),
             dma((2, 2, 2, 4, 2)),
-            dma((2, 2, 2, 4, 2)),
+            dma((2,)),
             dma((2,)),
             dma((2,)),
             dma((2, ZS)),
-            dma((2, ZS)),
-            dma((2,)),
-            dma((2,)),
-            dma((2,)),
-            dma((2, 2, 3, blocks)),
+            dma((2,)),
+            dma((2,)),
+            dma((2,)),
+            dma((2, 2)),
             dma((2, 2, blocks)),
-            dma((2, slots)),
+            dma((2,)),
             dma((2, layers)),
         ],
         compiler_params=pltpu.CompilerParams(

time: 148 us -> 131 us (0.89)
  Pallas kernels: 144 us -> 127 us
    pallas_call x1, Pallas kernels: 144 us -> 127 us  [shards(): pl.pallas_call(functools.partial(step_kernel, layers), out_shape=(jax.Sha...]
where the time goes in v3:
time: 131 us
  Pallas kernels  127 us (97%)
  local copies, waits for them, and re-layouts  3.14 us (2%)
    pallas_call x1, Pallas kernels, shards(): pl.pallas_call(functools.partial(step_kernel, layers), out_shape=(jax.Sha...  127 us
    unnamed x2, local copies, waits for them, and re-layouts  3.14 us

profile of v3, /device:TPU:31, one launch (start us, length us, event | category | flops | bytes accessed | tf_op | source)
XLA Modules:
  0.0 131.0 jit_solution(4102726776058092119)
XLA Ops:
  0.6 127.2 %transcoder_step.1 = (bf16[256,256]{1,0:T(8,128)(2,1)}, f32[256,128]{1,0:T(8,128)}) custom-call(bf16[256,256]{1,0:T(8,128)(2,1)} %bitcast.8, bf16[256,256]{1,0:T(8,128)(2,1)} %bitcast.9, bf16[4096,128]{1,0:T(8,128)(2,1)} %bitcast.7, f32[1,128]{1,0:T(1,128)} %enc_bias_ref.1, bf16[1152,4096]{1,0:T(8,128)(2,1)} %bitcast.6, f32[1,4096]{1,0:T(1,128)} %dec_bias_ref.1), custom_call_target="tpu_custom_call" | custom-call | tf_op jit(solution)/shard_map/transcoder_step/pallas_call | solution.py:562
  127.9 1.6 %copy.10 = bf16[1,256,256]{2,1,0:T(8,128)(2,1)} copy(bf16[1,256,256]{2,1,0:T(8,128)(2,1)} %bitcast.11) | data formatting | bytes 262144
  129.4 1.6 %copy.11 = f32[1,256,128]{2,1,0:T(8,128)} copy(f32[1,256,128]{2,1,0:T(8,128)} %bitcast.10) | data formatting | bytes 262144

commit v4 on v3

--- a/solution.py
+++ b/solution.py
@@ -11,7 +11,7 @@
 MESH = pl.DeviceIdType.MESH
 ZS = 8
 FEAT = ("z", "xl")
-ORDER = 25 * "AB" + "BAB"
+ORDER = 11 * "AB" + "AABB" + 12 * "AB" + "BAB"
 
 
 def around(v, step):
@@ -81,6 +81,10 @@
 
 
 class Narrow(Gather):
+    def begin(self):
+        for way in (0, 1):
+            self.push(way, self.own)
+
     def blocks(self, d):
         if d == 4:
             return [(None, 2 * around(self.z, 4) + self.xl)]
@@ -92,6 +96,8 @@
 
     def step(self, d):
         out = []
+        if d == 1:
+            self.push(2, self.own)
         if d < 5:
             for way, block in self.blocks(d):
                 self.arrive(block)
@@ -157,6 +163,7 @@
     res_send,
     res_recv,
     code_send,
+    relay_send,
     code_recv,
     ring_send,
     ring_recv,
@@ -238,13 +245,33 @@
         codes[h] = jnp.maximum(preact[h], 0.0).astype(bf16)
 
         def code_copy(k):
-            row = lax.rem(me + k, layers)
+            chip = lax.rem(me // 2 + k, half)
+            row = 2 * chip + jnp.where(heavy, 1, 0)
             wanted, slot = needs(row, me, layers)
+            wanted = wanted & (row != me)
             slot = jnp.where(wanted, slot, 0)
-            copy = remote(codes.at[h], code_slots.at[h, slot], code_send.at[h, k], code_recv.at[h], layer=row)
+            copy = remote(codes.at[h], code_slots.at[h, slot], code_send.at[h, k], code_recv.at[h, slot], layer=row)
             return wanted, copy
 
-        for k in range(1, layers):
+        def code_relay(n):
+            source = n + half * (1 - turn)
+            here, slot = needs(me, source, layers)
+            here = here & (source != me)
+            slot = jnp.where(here, slot, 0)
+            partner = me + 1 - 2 * turn
+            there, far = needs(partner, source, layers)
+            there = here & there & (source != partner)
+            far = jnp.where(there, far, 0)
+            copy = remote(
+                code_slots.at[h, slot], code_slots.at[h, far], relay_send.at[h, n], code_recv.at[h, far], layer=partner
+            )
+            return here, slot, there, copy
+
+        def code_wait(slot):
+            at = code_slots.at[h, slot]
+            return remote(at, at, code_send.at[h, 0], code_recv.at[h, slot], layer=mirror).wait_recv
+
+        for k in range(half):
             wanted, copy = code_copy(k)
             pl.when(wanted)(copy.start)
 
@@ -257,8 +284,15 @@
             code_slots[h, slots - 1] = jnp.zeros((tokens, feats), bf16)
 
         yield
-        got = code_slots.at[h, pl.ds(0, half)]
-        remote(got, got, code_send.at[h, 0], code_recv.at[h], layer=mirror).wait_recv()
+        for n in range(half):
+            arrived, slot, there, copy = code_relay(n)
+            pl.when(arrived)(code_wait(slot))
+            pl.when(there)(copy.start)
+        for n in range(half):
+            source = n + half * turn
+            arrived, slot = needs(me, source, layers)
+            arrived = arrived & (source != me)
+            pl.when(arrived)(code_wait(jnp.where(arrived, slot, 0)))
         for j in range(slots):
             cols = pl.ds(j * feats, feats)
             block = code_slots[h, j]
@@ -447,7 +481,7 @@
 
         grad_ref[here, :] = jnp.zeros((tokens, feats), f32)
         early, late = first.phases(), second.phases()
-        for phase in early[:3]:
+        for phase in early[:2]:
             phase()
             yield
 
@@ -457,15 +491,15 @@
             second.begin()
 
         yield
+        early[2]()
+        yield
+
+        @on_heavy
+        def _():
+            late[0]()
+
+        yield
         early[3]()
-        yield
-
-        @on_heavy
-        def _():
-            late[0]()
-
-        yield
-        early[4]()
         yield
 
         @on_heavy
@@ -474,13 +508,15 @@
             backward(1, [second.own] + second.ready(0) + second.ready(1), True, False)
 
         yield
+        early[4]()
+        yield
+
+        @on_heavy
+        def _():
+            late[2]()
+
+        yield
         backward(0, list(range(2 * ZS)), True, True)
-        yield
-
-        @on_heavy
-        def _():
-            late[2]()
-
         yield
 
         @on_heavy
@@ -512,9 +548,11 @@
 
         def drain():
             inputs.drain()
-            for k in range(1, layers):
+            for k in range(half):
                 wanted, copy = code_copy(k)
                 pl.when(wanted)(copy.wait_send)
+                _, _, there, copy = code_relay(k)
+                pl.when(there)(copy.wait_send)
 
             def drain_sums(a):
                 sent = residual.at[h, pl.ds(0, 14 if wide else 7)]
@@ -562,8 +600,8 @@
     error, grad = pl.pallas_call(
         functools.partial(step_kernel, layers),
         out_shape=(
-            jax.ShapeDtypeStruct((tokens, width), bf16),
-            jax.ShapeDtypeStruct((tokens, feats), f32),
+            vmem((tokens, width), bf16),
+            vmem((tokens, feats), f32),
         ),
         in_specs=[pl.BlockSpec(memory_space=pltpu.HBM)] * 6,
         out_specs=(pl.BlockSpec(memory_space=vmem),) * 2,
@@ -594,8 +632,9 @@
             dma((7,)),
             dma((2,)),
             dma((2, blocks)),
-            dma((2, layers)),
-            dma((2,)),
+            dma((2, layers // 2)),
+            dma((2, layers // 2)),
+            dma((2, slots)),
             dma((2, 2)),
             dma((2, 2, 2, 4, 2)),
             dma((2,)),

time: 131 us -> 122 us (0.931); the launches traced: 131 us -> 120 us
  Pallas kernels: 127 us -> 118 us
  local copies, waits for them, and re-layouts: 3.14 us -> 1.31 us
    pallas_call x1, Pallas kernels: 127 us -> 118 us  [shards(): pl.pallas_call(functools.partial(step_kernel, layers), out_shape=(vmem((t...]
    unnamed x2, local copies, waits for them, and re-layouts: 3.14 us -> 1.31 us
where the time goes in v4:
time: 122 us; the launch traced here: 120 us
  Pallas kernels  118 us (97%)
  local copies, waits for them, and re-layouts  1.31 us (1%)
    pallas_call x1, Pallas kernels, shards(): pl.pallas_call(functools.partial(step_kernel, layers), out_shape=(vmem((t...  118 us

profile of v4, /device:TPU:31, one launch (start us, length us, event | category | flops | bytes accessed | tf_op | source)
XLA Modules:
  0.0 120.2 jit_solution(4807015862512440718)
XLA Ops:
  0.6 118.3 %transcoder_step.1 = (bf16[256,256]{1,0:T(8,128)(2,1)S(1)}, f32[256,128]{1,0:T(8,128)S(1)}) custom-call(bf16[256,256]{1,0:T(8,128)(2,1)} %bitcast.10, bf16[256,256]{1,0:T(8,128)(2,1)} %bitcast.11, bf16[4096,128]{1,0:T(8,128)(2,1)} %bitcast.9, f32[1,128]{1,0:T(1,128)} %enc_bias_ref.1, bf16[1152,4096]{1,0:T(8,128)(2,1)} %bitcast.8, f32[1,4096]{1,0:T(1,128)} %dec_bias_ref.1), custom_call_target="tpu_custom_call" | custom-call | tf_op jit(solution)/shard_map/transcoder_step/pallas_call | solution.py:600
  118.9 0.7 copy.10
  119.6 0.7 copy.11

commit v5 on v4

--- a/solution.py
+++ b/solution.py
@@ -82,7 +82,7 @@
 
 class Narrow(Gather):
     def begin(self):
-        for way in (0, 1):
+        for way in (0, 1, 2):
             self.push(way, self.own)
 
     def blocks(self, d):
@@ -96,8 +96,6 @@
 
     def step(self, d):
         out = []
-        if d == 1:
-            self.push(2, self.own)
         if d < 5:
             for way, block in self.blocks(d):
                 self.arrive(block)

time: 122 us -> 121 us (level); the launches traced: 120 us -> 121 us
  no operation moved by 1% of the time
where the time goes in v5:
time: 121 us
  Pallas kernels  119 us (98%)
  local copies, waits for them, and re-layouts  1.31 us (1%)
    pallas_call x1, Pallas kernels, shards(): pl.pallas_call(functools.partial(step_kernel, layers), out_shape=(vmem((t...  119 us

profile of v5, /device:TPU:31, one launch (start us, length us, event | category | flops | bytes accessed | tf_op | source)
XLA Modules:
  0.0 121.4 jit_solution(15739085070942887640)
XLA Ops:
  0.6 119.4 %transcoder_step.1 = (bf16[256,256]{1,0:T(8,128)(2,1)S(1)}, f32[256,128]{1,0:T(8,128)S(1)}) custom-call(bf16[256,256]{1,0:T(8,128)(2,1)} %bitcast.10, bf16[256,256]{1,0:T(8,128)(2,1)} %bitcast.11, bf16[4096,128]{1,0:T(8,128)(2,1)} %bitcast.9, f32[1,128]{1,0:T(1,128)} %enc_bias_ref.1, bf16[1152,4096]{1,0:T(8,128)(2,1)} %bitcast.8, f32[1,4096]{1,0:T(1,128)} %dec_bias_ref.1), custom_call_target="tpu_custom_call" | custom-call | tf_op jit(solution)/shard_map/transcoder_step/pallas_call | solution.py:598
  120.0 0.7 copy.10
  120.7 0.7 copy.11
